TPU v7x, 128 devices: a whole 4x4x4 slice. The times are simulated.
128 devices in a mesh: grid: 8 (over z, core), dom: 16 (over y, x).
Axes of the slice: x: 4, y: 4, z: 4, core: 2. Of those that a mesh axis runs over, the one named last changes fastest.
Arguments:
- columns: bfloat16 [262144, 128], P(('grid', 'dom')), may hold values from -6 to 6
- column_live: int32 [262144], P(('grid', 'dom')), may hold values 0 or 1
- col_weight: float32 [262144], P(('grid', 'dom')), may hold values from 0.2 to 1
- col_slot: int32 [262144], P(('grid', 'dom')), may hold values from 0 to 511
- node_static: bfloat16 [65536, 256], P(('grid', 'dom')), may hold values from -6 to 6
- boundary_idx: int32 [32768], P(('grid', 'dom')), may hold values from 0 to 511
- edge_src: int32 [262144], P(('grid', 'dom')), may hold values from 0 to 1535
- edge_dst: int32 [262144], P(('grid', 'dom')), may hold values from 0 to 511
- edge_live: int32 [262144], P(('grid', 'dom')), may hold values from 0 to 1, as said below
- edge_weight: float32 [262144], P(('grid', 'dom')), may hold values from 0.2 to 1
- enc_in: bfloat16 [128, 256], replicated, may hold values from -0.5 to 0.5
- enc_out: bfloat16 [256, 256], replicated, may hold values from -0.375 to 0.375
- src_proj: bfloat16 [2, 256, 256], replicated, may hold values from -0.375 to 0.375
- dst_proj: bfloat16 [2, 256, 256], replicated, may hold values from -0.375 to 0.375
- msg_proj: bfloat16 [2, 256, 256], replicated, may hold values from -0.375 to 0.375
- node_cotangent: bfloat16 [65536, 256], P(('grid', 'dom')), may hold values from -6 to 6
Outputs:
- node_out: bfloat16 [65536, 256], P(('grid', 'dom'))
- enc_in_grad: float32 [128, 256], replicated
- enc_out_grad: float32 [256, 256], replicated
- src_grad: float32 [2, 256, 256], replicated
- dst_grad: float32 [2, 256, 256], replicated
- msg_grad: float32 [2, 256, 256], replicated
Inputs may be any that keep to these rules, and one draw needn't show every extreme that they name: `col_slot`: column slot j of a partition, with k * 16 <= j < (k + 1) * 16, is bound for partition k. `edge_live`: in each partition the live edge slots come first; some partition has all 2048 live.
All inputs are finite; a program needn't handle non-finite values. No bound on the sum of `column_live` on one device may be relied on, other than what follows from the above.
Results may differ from a plain program's by a relative error of at most 0.0095.
Values may be sent and summed in bfloat16 or wider, within the bound.
A program may use at most 128 MiB of HBM per device.

v0:
```python
import jax
import jax.numpy as jnp
from jax import lax
from jax.sharding import PartitionSpec as P


def extended(shard, sides, width):
    edges = {}
    for axis, dim in sides:
        count, length = (lax.axis_size(axis), shard.shape[dim])
        up = [(i, (i + 1) % count) for i in range(count - 1)]
        last = lax.slice_in_dim(shard, length - width, length, axis=dim)
        initial = lax.slice_in_dim(shard, 0, width, axis=dim)
        edges[dim] = (
            lax.ppermute(last, axis, up),
            lax.ppermute(initial, axis, [(b, a) for a, b in up]),
        )
    done = []
    for _, dim in sides:
        low, high = edges[dim]
        around = [(width, width) if d in done else (0, 0) for d in range(shard.ndim)]
        shard = jnp.concatenate([jnp.pad(low, around), shard, jnp.pad(high, around)], axis=dim)
        done.append(dim)
    return shard


def passed_along(shard, axis, by):
    count = lax.axis_size(axis)
    pairs = [(i, i + by) for i in range(count) if 0 <= i + by < count]
    return lax.ppermute(shard, axis, pairs)


def silu_grad(inputs):
    sigmoid_val = jax.nn.sigmoid(inputs)
    return sigmoid_val * (1.0 + inputs * (1.0 - sigmoid_val))


def outer_sum(left_side, right_side):
    return lax.dot_general(
        left_side, right_side, (((0,), (0,)), ((), ())), preferred_element_type=jnp.float32
    )


def times_transpose(left_side, right_side):
    return lax.dot_general(
        left_side, right_side, (((1,), (1,)), ((), ())), preferred_element_type=jnp.float32
    )


def per_device(
    columns,
    column_live,
    col_weight,
    col_slot,
    node_static,
    boundary_idx,
    edge_src,
    edge_dst,
    edge_live,
    edge_weight,
    enc_in,
    enc_out,
    src_proj,
    dst_proj,
    msg_proj,
    node_cotangent,
):
    peer_count = lax.axis_size(("grid", "dom"))
    col_count = columns.shape[0]
    node_count = node_static.shape[0]
    feat_width = enc_out.shape[1]
    bucket = col_count // peer_count
    layer_count = src_proj.shape[0]
    col_scale = col_weight * column_live.astype(jnp.float32)
    edge_scale = edge_weight * edge_live.astype(jnp.float32)
    enc_pre = jnp.dot(columns, enc_in, preferred_element_type=jnp.float32)
    enc_act = jax.nn.silu(enc_pre).astype(jnp.bfloat16)
    col_embed = (
        jnp.dot(enc_act, enc_out, preferred_element_type=jnp.float32) * col_scale[:, None]
    ).astype(jnp.bfloat16)
    recv_rows, recv_slots = (
        lax.all_to_all(
            col_embed.reshape(peer_count, bucket, feat_width),
            ("grid", "dom"),
            split_axis=0,
            concat_axis=0,
            tiled=True,
        ),
        lax.all_to_all(
            col_slot.reshape(peer_count, bucket),
            ("grid", "dom"),
            split_axis=0,
            concat_axis=0,
            tiled=True,
        ),
    )
    flat_slots = recv_slots.reshape(col_count)
    pooled = jax.ops.segment_sum(
        recv_rows.reshape(col_count, feat_width).astype(jnp.float32),
        flat_slots,
        num_segments=node_count,
    )
    node_state = (node_static.astype(jnp.float32) + pooled).astype(jnp.bfloat16)
    stored = []
    for layer_idx in range(layer_count):
        rim_rows = node_state[boundary_idx]
        padded = extended(rim_rows[None, None], (("grid", 0), ("dom", 1)), 1)
        src_table = jnp.concatenate(
            [node_state, padded[0, 1], padded[2, 1], padded[1, 0], padded[1, 2]], 0
        )
        from_src = jnp.dot(src_table, src_proj[layer_idx], preferred_element_type=jnp.float32)
        from_dst = jnp.dot(node_state, dst_proj[layer_idx], preferred_element_type=jnp.float32)
        pre_edge = from_src[edge_src] + from_dst[edge_dst]
        act_edge = jax.nn.silu(pre_edge).astype(jnp.bfloat16)
        message = (
            jnp.dot(act_edge, msg_proj[layer_idx], preferred_element_type=jnp.float32)
            * edge_scale[:, None]
        )
        gathered = jax.ops.segment_sum(message, edge_dst, num_segments=node_count)
        stored.append((node_state, src_table, pre_edge, act_edge))
        node_state = (node_state.astype(jnp.float32) + gathered).astype(jnp.bfloat16)
    grad_state = node_cotangent.astype(jnp.float32)
    layer_terms = [None] * layer_count
    for layer_idx in reversed(range(layer_count)):
        own_rows, src_table, pre_edge, act_edge = stored[layer_idx]
        grad_msg = (grad_state[edge_dst] * edge_scale[:, None]).astype(jnp.bfloat16)
        msg_term = outer_sum(act_edge, grad_msg)
        grad_act = times_transpose(grad_msg, msg_proj[layer_idx])
        grad_pre = grad_act * silu_grad(pre_edge)
        grad_src = jax.ops.segment_sum(grad_pre, edge_src, num_segments=src_table.shape[0]).astype(
            jnp.bfloat16
        )
        grad_dst = jax.ops.segment_sum(grad_pre, edge_dst, num_segments=node_count).astype(
            jnp.bfloat16
        )
        src_term = outer_sum(src_table, grad_src)
        dst_term = outer_sum(own_rows, grad_dst)
        grad_table = times_transpose(grad_src, src_proj[layer_idx])
        rim_sends = grad_table[node_count:].reshape(4, boundary_idx.shape[0], feat_width)
        from_upper = passed_along(rim_sends[0].astype(jnp.bfloat16), "grid", -1).astype(jnp.float32)
        from_lower = passed_along(rim_sends[1].astype(jnp.bfloat16), "grid", 1).astype(jnp.float32)
        from_right = passed_along(rim_sends[2].astype(jnp.bfloat16), "dom", -1).astype(jnp.float32)
        from_left = passed_along(rim_sends[3].astype(jnp.bfloat16), "dom", 1).astype(jnp.float32)
        rim_grad = from_upper + from_lower + from_right + from_left
        grad_state = (
            grad_state
            + grad_table[:node_count]
            + times_transpose(grad_dst, dst_proj[layer_idx])
            + jax.ops.segment_sum(rim_grad, boundary_idx, num_segments=node_count)
        )
        layer_terms_now = (src_term, dst_term, msg_term)
        layer_terms[layer_idx] = layer_terms_now
    grad_nodes = grad_state.astype(jnp.bfloat16)
    back_rows = grad_nodes[flat_slots].reshape(peer_count, bucket, feat_width)
    grad_embed = lax.all_to_all(
        back_rows, ("grid", "dom"), split_axis=0, concat_axis=0, tiled=True
    ).reshape(col_count, feat_width)
    grad_enc = (grad_embed.astype(jnp.float32) * col_scale[:, None]).astype(jnp.bfloat16)
    out_term = outer_sum(enc_act, grad_enc)
    grad_hidden = times_transpose(grad_enc, enc_out)
    grad_enc_pre = (grad_hidden * silu_grad(enc_pre)).astype(jnp.bfloat16)
    in_term = outer_sum(columns, grad_enc_pre)
    src_grad = jnp.stack([entry[0] for entry in layer_terms], 0)
    dst_grad = jnp.stack([entry[1] for entry in layer_terms], 0)
    msg_grad = jnp.stack([entry[2] for entry in layer_terms], 0)
    enc_in_grad, enc_out_grad, src_grad, dst_grad, msg_grad = lax.psum(
        (in_term, out_term, src_grad, dst_grad, msg_grad), ("grid", "dom")
    )
    return (node_state, enc_in_grad, enc_out_grad, src_grad, dst_grad, msg_grad)


def solution(mesh):
    placed = (
        P(("grid", "dom"), None),
        P(("grid", "dom")),
        P(("grid", "dom")),
        P(("grid", "dom")),
        P(("grid", "dom"), None),
        P(("grid", "dom")),
        P(("grid", "dom")),
        P(("grid", "dom")),
        P(("grid", "dom")),
        P(("grid", "dom")),
        P(),
        P(),
        P(),
        P(),
        P(),
        P(("grid", "dom"), None),
    )
    return jax.shard_map(
        per_device,
        mesh=mesh,
        in_specs=placed,
        out_specs=(P(("grid", "dom"), None), P(), P(), P(), P(), P()),
        check_vma=False,
    )
```

profile of v0, /device:TPU:1, one launch (start us, length us, event | category | flops | bytes accessed | tf_op | source)
XLA Modules:
  0.0 472.0 jit_solution(3878509830577589204)
XLA Ops:
  8.6 11.5 %all-to-all-start = ((s32[128,1,16]{2,1,0:T(1,128)}), s32[128,1,16]{2,1,0:T(1,128)S(1)}, u32[]{:S(2)}, u32[]{:S(2)}) async-start(s32[128,1,16]{2,1,0:T(1,128)} %bitcast), calls=%async_computation | async-start | bytes 131072 | tf_op jit(solution)/shard_map/all_to_all | solution.py:89
  26.1 3.5 all-to-all-done
  29.7 6.2 %all-to-all-start.1 = ((bf16[128,16,256]{2,1,0:T(8,128)(2,1)}), bf16[128,16,256]{2,1,0:T(8,128)(2,1)S(1)}, u32[]{:S(2)}, u32[]{:S(2)}) async-start(bf16[128,16,256]{2,1,0:T(8,128)(2,1)} %bitcast.1), calls=%async_computation.1 | async-start | bytes 2097152 | tf_op jit(solution)/shard_map/all_to_all | solution.py:82
  36.1 8.6 %gather_fusion.6 = f32[2048,256]{1,0:T(8,128)} fusion(f32[512,256]{1,0:T(8,128)S(1)} %convert_element_type.129, s32[2048]{0:T(1024)S(1)} %get-tuple-element.48), kind=kCustom, calls=%fused_computation.6 | custom fusion | bytes 4202496 | tf_op jit(solution)/shard_map/gather | solution.py:126
  46.9 7.9 %all-to-all-done.1 = bf16[128,16,256]{2,1,0:T(8,128)(2,1)S(1)} async-done(((bf16[128,16,256]{2,1,0:T(8,128)(2,1)}), bf16[128,16,256]{2,1,0:T(8,128)(2,1)S(1)}, u32[]{:S(2)}, u32[]{:S(2)}) %all-to-all-start.1) | async-done | bytes 1048608 | tf_op jit(solution)/shard_map/all_to_all | solution.py:82
  54.8 11.8 %scatter_custom_fusion = f32[512,256]{1,0:T(8,128)S(1)} fusion(f32[512,256]{1,0:T(8,128)S(1)} %convert_element_type.115, s32[2048]{0:T(1024)S(1)} %reshape.157, bf16[2048,256]{1,0:T(8,128)(2,1)S(1)} %bitcast.99), kind=kCustom, calls=%fused_computation.28 | custom fusion | flops 1048576 | bytes 1572864 | tf_op jit(solution)/shard_map/scatter-add | solution.py:98
  69.8 4.0 collective-permute-start.2
  73.8 3.7 collective-permute-start.1
  80.2 8.6 %gather_fusion.2 = f32[2048,256]{1,0:T(8,128)} fusion(f32[512,256]{1,0:T(8,128)S(1)} %fusion.51, s32[2048]{0:T(1024)S(1)} %get-tuple-element.48), kind=kCustom, calls=%fused_computation.2 | custom fusion | bytes 4202496 | tf_op jit(solution)/shard_map/gather | solution.py:113
  93.0 8.6 %gather_fusion.1 = f32[2048,256]{1,0:T(8,128)} fusion(f32[1536,256]{1,0:T(8,128)S(1)} %fusion.56, s32[2048]{0:T(1024)S(1)} %get-tuple-element.47), kind=kCustom, calls=%fused_computation.1 | custom fusion | bytes 4202496 | tf_op jit(solution)/shard_map/gather | solution.py:113
  107.2 12.4 %scatter_fusion = f32[512,256]{1,0:T(8,128)S(1)} fusion(f32[512,256]{1,0:T(8,128)S(1)} %convert_element_type.122, s32[2048]{0:T(1024)S(1)} %copy-done.38, f32[2048,256]{1,0:T(8,128)} %convolution_multiply_fusion.4), kind=kCustom, calls=%fused_computation.10 | custom fusion | flops 524288 | bytes 6299648 | tf_op jit(solution)/shard_map/scatter-add | solution.py:119
  122.4 4.0 collective-permute-start.6
  132.2 8.6 %gather_fusion.5 = f32[2048,256]{1,0:T(8,128)} fusion(f32[512,256]{1,0:T(8,128)S(1)} %fusion.42, s32[2048]{0:T(1024)S(1)} %get-tuple-element.48), kind=kCustom, calls=%fused_computation.5 | custom fusion | bytes 4202496 | tf_op jit(solution)/shard_map/gather | solution.py:113
  142.3 9.3 %gather_fusion.4 = f32[2048,256]{1,0:T(8,128)} fusion(f32[1536,256]{1,0:T(8,128)S(1)} %fusion.45, s32[2048]{0:T(1024)} %copy-done.40), kind=kCustom, calls=%fused_computation.4 | custom fusion | bytes 4202496 | tf_op jit(solution)/shard_map/gather | solution.py:113
  151.6 3.9 multiply_convert_fusion.2
  159.4 12.4 %scatter_custom_fusion.4 = f32[512,256]{1,0:T(8,128)} fusion(s32[2048]{0:T(1024)} %param.23, f32[2048,256]{1,0:T(8,128)S(1)} %convolution_multiply_fusion.2, f32[]{:T(128)} %constant.9.clone.1), kind=kCustom, calls=%fused_computation.82 | custom fusion | flops 524288 | bytes 524800 | tf_op jit(solution)/shard_map/scatter-add | solution.py:133
  171.9 12.4 %scatter_custom_fusion.3 = f32[1536,256]{1,0:T(8,128)S(1)} fusion(s32[2048]{0:T(1024)} %param.22, f32[2048,256]{1,0:T(8,128)} %copy-done.47, f32[]{:T(128)} %constant.9.clone.1), kind=kCustom, calls=%fused_computation.50 | custom fusion | flops 524288 | bytes 1573376 | tf_op jit(solution)/shard_map/scatter-add | solution.py:130
  184.3 3.4 convolution_bitcast_fusion.2
  193.8 3.9 collective-permute-start.9
  203.5 8.6 %gather_fusion.7 = f32[2048,256]{1,0:T(8,128)} fusion(f32[512,256]{1,0:T(8,128)S(1)} %scatter_custom_fusion.5, s32[2048]{0:T(1024)S(1)} %get-tuple-element.48), kind=kCustom, calls=%fused_computation.7 | custom fusion | bytes 4202496 | tf_op jit(solution)/shard_map/gather | solution.py:126
  212.2 5.2 %convolution_multiply_fusion.1 = f32[2048,256]{1,0:T(8,128)} fusion(f32[2048,256]{1,0:T(8,128)} %gather_fusion.1, f32[2048,256]{1,0:T(8,128)} %gather_fusion.2, bf16[2,256,256]{2,1,0:T(8,128)(2,1)S(1)} %copy-done.28, f32[2048,256]{1,0:T(8,128)} %gather_fusion.7, f32[2048]{0:T(1024)S(1)} %convert_multiply_fusion.1), kind=kOutput, calls=%fused_computation.19 | convolution fusion | flops 274202624 | bytes 8527872 | tf_op jit(solution)/shard_map/dot_general | solution.py:45
  217.3 12.7 %scatter_custom_fusion.7 = f32[512,256]{1,0:T(8,128)} fusion(s32[2048]{0:T(1024)} %param.23, f32[2048,256]{1,0:T(8,128)} %convolution_multiply_fusion.1, f32[]{:T(128)} %constant.9.clone.1), kind=kCustom, calls=%fused_computation.80 | custom fusion | flops 524288 | bytes 524800 | tf_op jit(solution)/shard_map/scatter-add | solution.py:133
  230.1 12.4 %scatter_custom_fusion.6 = f32[1536,256]{1,0:T(8,128)S(1)} fusion(s32[2048]{0:T(1024)} %param.22, f32[2048,256]{1,0:T(8,128)} %convolution_multiply_fusion.1, f32[]{:T(128)} %constant.9.clone.1), kind=kCustom, calls=%fused_computation.48 | custom fusion | flops 524288 | bytes 1573376 | tf_op jit(solution)/shard_map/scatter-add | solution.py:130
  244.9 4.9 %collective-permute-start.15 = (bf16[256,256]{1,0:T(8,128)(2,1)S(1)}, bf16[256,256]{1,0:T(8,128)(2,1)S(1)}, u32[]{:S(2)}, u32[]{:S(2)}) collective-permute-start(bf16[256,256]{1,0:T(8,128)(2,1)S(1)} %get-tuple-element.34), channel_id=1, source_target_pairs={{0,1},{1,2},{2,3},{3,4},{4,5},{5,6},{6,7},{7,8},{8,9},{9,10},{10,1... | collective-permute-start | bytes 393224 | tf_op jit(solution)/shard_map/ppermute | solution.py:30
  251.1 4.9 %collective-permute-start.13 = (bf16[256,256]{1,0:T(8,128)(2,1)S(1)}, bf16[256,256]{1,0:T(8,128)(2,1)}, u32[]{:S(2)}, u32[]{:S(2)}) collective-permute-start(bf16[256,256]{1,0:T(8,128)(2,1)S(1)} %get-tuple-element.36), channel_id=1, source_target_pairs={{0,16},{16,32},{32,48},{48,64},{64,80},{80,96},{96,112},{1,17},{17... | collective-permute-start | bytes 393224 | tf_op jit(solution)/shard_map/ppermute | solution.py:30
  258.6 4.1 scatter_custom_fusion.8
  263.9 9.0 %gather_fusion.8 = bf16[2048,256]{1,0:T(8,128)(2,1)} fusion(bf16[512,256]{1,0:T(8,128)(2,1)S(1)} %convert_element_type.144, s32[2048]{0:T(1024)S(1)} %copy-done.41), kind=kCustom, calls=%fused_computation.8 | custom fusion | bytes 2105344 | tf_op jit(solution)/shard_map/gather | solution.py:154
  272.9 11.8 %all-to-all-start.2 = ((bf16[128,16,256]{2,1,0:T(8,128)(2,1)}), bf16[128,16,256]{2,1,0:T(8,128)(2,1)}, u32[]{:S(2)}, u32[]{:S(2)}) async-start(bf16[128,16,256]{2,1,0:T(8,128)(2,1)} %bitcast.100), calls=%async_computation.2 | async-start | bytes 2097152 | tf_op jit(solution)/shard_map/all_to_all | solution.py:155
  292.4 10.8 %all-to-all-done.2 = bf16[128,16,256]{2,1,0:T(8,128)(2,1)} async-done(((bf16[128,16,256]{2,1,0:T(8,128)(2,1)}), bf16[128,16,256]{2,1,0:T(8,128)(2,1)}, u32[]{:S(2)}, u32[]{:S(2)}) %all-to-all-start.2) | async-done | bytes 1048608 | tf_op jit(solution)/shard_map/all_to_all | solution.py:155
  306.0 3.4 fusion.6
  312.4 12.2 %scatter_fusion.1 = f32[512,256]{1,0:T(8,128)S(1)} fusion(f32[512,256]{1,0:T(8,128)S(1)} %convert_element_type.126, s32[2048]{0:T(1024)S(1)} %copy-done.39, f32[2048,256]{1,0:T(8,128)} %convolution_multiply_fusion.3), kind=kCustom, calls=%fused_computation.11 | custom fusion | flops 524288 | bytes 6299648 | tf_op jit(solution)/shard_map/scatter-add | solution.py:119
  325.3 132.5 %all-reduce.3.cloned.1.call-done = (f32[128,256]{0,1:T(8,128)}, f32[256,256]{1,0:T(8,128)}, f32[2,256,256]{2,1,0:T(8,128)}, f32[2,256,256]{2,1,0:T(8,128)}, f32[2,256,256]{2,1,0:T(8,128)}) async-done(((f32[128,256]{0,1:T(8,128)}, f32[256,256]{1,0:T(8,128)}, f32[2,256,256]{2,1,0:T(8,128)}, f32[2,256,256]{2,1,0:T(8,128)}, f32[2,256,256]{2,1,0:T(8,128)}), (f32[128,256]{0,1:T(8,128)}, f32[256,256]{1,0:T(8,128)}, ...) | async-done | bytes 1966096 | tf_op jit(solution)/shard_map/psum | solution.py:166
  (186 shorter events, 79.3 us)
Async XLA Ops:
  7.2 13.7 %copy-start = (bf16[2048,128]{1,0:T(8,128)(2,1)S(1)}, bf16[2048,128]{1,0:T(8,128)(2,1)}, u32[]{:S(2)}) copy-start(bf16[2048,128]{1,0:T(8,128)(2,1)} %param.16) | copy-start | bytes 1572868
  8.6 21.0 %all-to-all-start = ((s32[128,1,16]{2,1,0:T(1,128)}), s32[128,1,16]{2,1,0:T(1,128)S(1)}, u32[]{:S(2)}, u32[]{:S(2)}) async-start(s32[128,1,16]{2,1,0:T(1,128)} %bitcast), calls=%async_computation | async-start | bytes 131072 | tf_op jit(solution)/shard_map/all_to_all | solution.py:89
  24.7 11.3 %copy-start.13 = (bf16[512,256]{1,0:T(8,128)(2,1)S(1)}, bf16[512,256]{1,0:T(8,128)(2,1)}, u32[]{:S(2)}) copy-start(bf16[512,256]{1,0:T(8,128)(2,1)} %param.31) | copy-start | bytes 786436
  26.1 66.8 %copy-start.40 = (s32[2048]{0:T(1024)}, s32[2048]{0:T(1024)S(1)}, u32[]{:S(2)}) copy-start(s32[2048]{0:T(1024)S(1)} %get-tuple-element.47) | copy-start | bytes 24580
  29.7 25.1 %all-to-all-start.1 = ((bf16[128,16,256]{2,1,0:T(8,128)(2,1)}), bf16[128,16,256]{2,1,0:T(8,128)(2,1)S(1)}, u32[]{:S(2)}, u32[]{:S(2)}) async-start(bf16[128,16,256]{2,1,0:T(8,128)(2,1)} %bitcast.1), calls=%async_computation.1 | async-start | bytes 2097152 | tf_op jit(solution)/shard_map/all_to_all | solution.py:82
  44.7 35.2 %copy-start.42 = (s32[1024]{0:T(1024)}, s32[1024]{0:T(1024)S(1)}, u32[]{:S(2)}) copy-start(s32[1024]{0:T(1024)S(1)} %pad_clamp_fusion) | copy-start | bytes 12292
  54.8 25.2 %copy-start.18 = (bf16[2,256,256]{2,1,0:T(8,128)(2,1)S(1)}, bf16[2,256,256]{2,1,0:T(8,128)(2,1)}, u32[]{:S(2)}) copy-start(bf16[2,256,256]{2,1,0:T(8,128)(2,1)} %param.29) | copy-start | bytes 786436
  68.5 22.3 %collective-permute-start.3 = (bf16[1,1,256,256]{3,2,1,0:T(8,128)(2,1)S(1)}, bf16[1,1,256,256]{3,2,1,0:T(8,128)(2,1)S(1)}, u32[]{:S(2)}, u32[]{:S(2)}) collective-permute-start(bf16[1,1,256,256]{3,2,1,0:T(8,128)(2,1)S(1)} %bitcast.102), channel_id=1, source_target_pairs={{1,0},{2,1},{3,2},{4,3},{5,4},{6,5},{7,6},{8,7},{9,8},{10,9},{11,1... | collective-permute-start | bytes 393224 | tf_op jit(solution)/shard_map/ppermute | solution.py:16
  69.8 20.3 %collective-permute-start.2 = (bf16[1,1,256,256]{3,2,1,0:T(8,128)(2,1)S(1)}, bf16[1,1,256,256]{3,2,1,0:T(8,128)(2,1)S(1)}, u32[]{:S(2)}, u32[]{:S(2)}) collective-permute-start(bf16[1,1,256,256]{3,2,1,0:T(8,128)(2,1)S(1)} %bitcast.103), channel_id=1, source_target_pairs={{0,1},{1,2},{2,3},{3,4},{4,5},{5,6},{6,7},{7,8},{8,9},{9,10},{10,1... | collective-permute-start | bytes 393224 | tf_op jit(solution)/shard_map/ppermute | solution.py:15
  73.8 15.6 %collective-permute-start.1 = (bf16[1,1,256,256]{3,2,1,0:T(8,128)(2,1)S(1)}, bf16[1,1,256,256]{3,2,1,0:T(8,128)(2,1)S(1)}, u32[]{:S(2)}, u32[]{:S(2)}) collective-permute-start(bf16[1,1,256,256]{3,2,1,0:T(8,128)(2,1)S(1)} %bitcast.104), channel_id=1, source_target_pairs={{16,0},{32,16},{48,32},{64,48},{80,64},{96,80},{112,96},{17,1},{33... | collective-permute-start | bytes 393224 | tf_op jit(solution)/shard_map/ppermute | solution.py:16
  77.5 11.3 %collective-permute-start = (bf16[1,1,256,256]{3,2,1,0:T(8,128)(2,1)S(1)}, bf16[1,1,256,256]{3,2,1,0:T(8,128)(2,1)S(1)}, u32[]{:S(2)}, u32[]{:S(2)}) collective-permute-start(bf16[1,1,256,256]{3,2,1,0:T(8,128)(2,1)S(1)} %bitcast.105), channel_id=1, source_target_pairs={{0,16},{16,32},{32,48},{48,64},{64,80},{80,96},{96,112},{1,17},{17... | collective-permute-start | bytes 393224 | tf_op jit(solution)/shard_map/ppermute | solution.py:15
  119.6 12.4 %copy-start.19 = (bf16[2,256,256]{2,1,0:T(8,128)(2,1)S(1)}, bf16[2,256,256]{2,1,0:T(8,128)(2,1)}, u32[]{:S(2)}) copy-start(bf16[2,256,256]{2,1,0:T(8,128)(2,1)} %param.29) | copy-start | bytes 786436
  121.1 19.8 %collective-permute-start.7 = (bf16[1,1,256,256]{3,2,1,0:T(8,128)(2,1)S(1)}, bf16[1,1,256,256]{3,2,1,0:T(8,128)(2,1)S(1)}, u32[]{:S(2)}, u32[]{:S(2)}) collective-permute-start(bf16[1,1,256,256]{3,2,1,0:T(8,128)(2,1)S(1)} %bitcast.106), channel_id=1, source_target_pairs={{1,0},{2,1},{3,2},{4,3},{5,4},{6,5},{7,6},{8,7},{9,8},{10,9},{11,1... | collective-permute-start | bytes 393224 | tf_op jit(solution)/shard_map/ppermute | solution.py:16
  122.4 18.4 %collective-permute-start.6 = (bf16[1,1,256,256]{3,2,1,0:T(8,128)(2,1)S(1)}, bf16[1,1,256,256]{3,2,1,0:T(8,128)(2,1)S(1)}, u32[]{:S(2)}, u32[]{:S(2)}) collective-permute-start(bf16[1,1,256,256]{3,2,1,0:T(8,128)(2,1)S(1)} %bitcast.107), channel_id=1, source_target_pairs={{0,1},{1,2},{2,3},{3,4},{4,5},{5,6},{6,7},{7,8},{8,9},{9,10},{10,1... | collective-permute-start | bytes 393224 | tf_op jit(solution)/shard_map/ppermute | solution.py:15
  126.4 14.4 %collective-permute-start.5 = (bf16[1,1,256,256]{3,2,1,0:T(8,128)(2,1)S(1)}, bf16[1,1,256,256]{3,2,1,0:T(8,128)(2,1)S(1)}, u32[]{:S(2)}, u32[]{:S(2)}) collective-permute-start(bf16[1,1,256,256]{3,2,1,0:T(8,128)(2,1)S(1)} %bitcast.108), channel_id=1, source_target_pairs={{16,0},{32,16},{48,32},{64,48},{80,64},{96,80},{112,96},{17,1},{33... | collective-permute-start | bytes 393224 | tf_op jit(solution)/shard_map/ppermute | solution.py:16
  128.9 11.9 %collective-permute-start.4 = (bf16[1,1,256,256]{3,2,1,0:T(8,128)(2,1)S(1)}, bf16[1,1,256,256]{3,2,1,0:T(8,128)(2,1)S(1)}, u32[]{:S(2)}, u32[]{:S(2)}) collective-permute-start(bf16[1,1,256,256]{3,2,1,0:T(8,128)(2,1)S(1)} %bitcast.109), channel_id=1, source_target_pairs={{0,16},{16,32},{32,48},{48,64},{64,80},{80,96},{96,112},{1,17},{17... | collective-permute-start | bytes 393224 | tf_op jit(solution)/shard_map/ppermute | solution.py:15
  188.2 11.0 %collective-permute-start.8 = (bf16[256,256]{1,0:T(8,128)(2,1)S(1)}, bf16[256,256]{1,0:T(8,128)(2,1)S(1)}, u32[]{:S(2)}, u32[]{:S(2)}) collective-permute-start(bf16[256,256]{1,0:T(8,128)(2,1)S(1)} %get-tuple-element.37), channel_id=1, source_target_pairs={{16,0},{32,16},{48,32},{64,48},{80,64},{96,80},{112,96},{17,1},{33... | collective-permute-start | bytes 393224 | tf_op jit(solution)/shard_map/ppermute | solution.py:30
  190.2 9.0 %collective-permute-start.11 = (bf16[256,256]{1,0:T(8,128)(2,1)S(1)}, bf16[256,256]{1,0:T(8,128)(2,1)S(1)}, u32[]{:S(2)}, u32[]{:S(2)}) collective-permute-start(bf16[256,256]{1,0:T(8,128)(2,1)S(1)} %get-tuple-element.38), channel_id=1, source_target_pairs={{0,1},{1,2},{2,3},{3,4},{4,5},{5,6},{6,7},{7,8},{8,9},{9,10},{10,1... | collective-permute-start | bytes 393224 | tf_op jit(solution)/shard_map/ppermute | solution.py:30
  192.5 6.7 %collective-permute-start.10 = (bf16[256,256]{1,0:T(8,128)(2,1)S(1)}, bf16[256,256]{1,0:T(8,128)(2,1)S(1)}, u32[]{:S(2)}, u32[]{:S(2)}) collective-permute-start(bf16[256,256]{1,0:T(8,128)(2,1)S(1)} %get-tuple-element.39), channel_id=1, source_target_pairs={{1,0},{2,1},{3,2},{4,3},{5,4},{6,5},{7,6},{8,7},{9,8},{10,9},{11,1... | collective-permute-start | bytes 393224 | tf_op jit(solution)/shard_map/ppermute | solution.py:30
  193.8 6.7 %collective-permute-start.9 = (bf16[256,256]{1,0:T(8,128)(2,1)S(1)}, bf16[256,256]{1,0:T(8,128)(2,1)}, u32[]{:S(2)}, u32[]{:S(2)}) collective-permute-start(bf16[256,256]{1,0:T(8,128)(2,1)S(1)} %get-tuple-element.40), channel_id=1, source_target_pairs={{0,16},{16,32},{32,48},{48,64},{64,80},{80,96},{96,112},{1,17},{17... | collective-permute-start | bytes 393224 | tf_op jit(solution)/shard_map/ppermute | solution.py:30
  242.4 13.6 %copy-start.5 = (f32[512,256]{1,0:T(8,128)S(1)}, f32[512,256]{1,0:T(8,128)}, u32[]{:S(2)}) copy-start(f32[512,256]{1,0:T(8,128)} %scatter_custom_fusion.7) | copy-start | bytes 1572868
  242.5 13.6 %copy-start.21 = (bf16[2,256,256]{2,1,0:T(8,128)(2,1)S(1)}, bf16[2,256,256]{2,1,0:T(8,128)(2,1)}, u32[]{:S(2)}) copy-start(bf16[2,256,256]{2,1,0:T(8,128)(2,1)} %param.29) | copy-start | bytes 786436
  242.9 20.9 %copy-start.41 = (s32[2048]{0:T(1024)S(1)}, s32[2048]{0:T(1024)}, u32[]{:S(2)}) copy-start(s32[2048]{0:T(1024)} %broadcast_clamp_fusion) | copy-start | bytes 24580
  242.9 14.2 %collective-permute-start.12 = (bf16[256,256]{1,0:T(8,128)(2,1)S(1)}, bf16[256,256]{1,0:T(8,128)(2,1)S(1)}, u32[]{:S(2)}, u32[]{:S(2)}) collective-permute-start(bf16[256,256]{1,0:T(8,128)(2,1)S(1)} %get-tuple-element.33), channel_id=1, source_target_pairs={{16,0},{32,16},{48,32},{64,48},{80,64},{96,80},{112,96},{17,1},{33... | collective-permute-start | bytes 393224 | tf_op jit(solution)/shard_map/ppermute | solution.py:30
  244.9 12.2 %collective-permute-start.15 = (bf16[256,256]{1,0:T(8,128)(2,1)S(1)}, bf16[256,256]{1,0:T(8,128)(2,1)S(1)}, u32[]{:S(2)}, u32[]{:S(2)}) collective-permute-start(bf16[256,256]{1,0:T(8,128)(2,1)S(1)} %get-tuple-element.34), channel_id=1, source_target_pairs={{0,1},{1,2},{2,3},{3,4},{4,5},{5,6},{6,7},{7,8},{8,9},{9,10},{10,1... | collective-permute-start | bytes 393224 | tf_op jit(solution)/shard_map/ppermute | solution.py:30
  249.8 8.2 %collective-permute-start.14 = (bf16[256,256]{1,0:T(8,128)(2,1)S(1)}, bf16[256,256]{1,0:T(8,128)(2,1)S(1)}, u32[]{:S(2)}, u32[]{:S(2)}) collective-permute-start(bf16[256,256]{1,0:T(8,128)(2,1)S(1)} %get-tuple-element.35), channel_id=1, source_target_pairs={{1,0},{2,1},{3,2},{4,3},{5,4},{6,5},{7,6},{8,7},{9,8},{10,9},{11,1... | collective-permute-start | bytes 393224 | tf_op jit(solution)/shard_map/ppermute | solution.py:30
  251.1 7.6 %collective-permute-start.13 = (bf16[256,256]{1,0:T(8,128)(2,1)S(1)}, bf16[256,256]{1,0:T(8,128)(2,1)}, u32[]{:S(2)}, u32[]{:S(2)}) collective-permute-start(bf16[256,256]{1,0:T(8,128)(2,1)S(1)} %get-tuple-element.36), channel_id=1, source_target_pairs={{0,16},{16,32},{32,48},{48,64},{64,80},{80,96},{96,112},{1,17},{17... | collective-permute-start | bytes 393224 | tf_op jit(solution)/shard_map/ppermute | solution.py:30
  272.9 12.1 %copy-start.8 = (f32[512,256]{1,0:T(8,128)S(1)}, f32[512,256]{1,0:T(8,128)}, u32[]{:S(2)}) copy-start(f32[512,256]{1,0:T(8,128)} %scatter_custom_fusion.4) | copy-start | bytes 1572868
  272.9 30.3 %all-to-all-start.2 = ((bf16[128,16,256]{2,1,0:T(8,128)(2,1)}), bf16[128,16,256]{2,1,0:T(8,128)(2,1)}, u32[]{:S(2)}, u32[]{:S(2)}) async-start(bf16[128,16,256]{2,1,0:T(8,128)(2,1)} %bitcast.100), calls=%async_computation.2 | async-start | bytes 2097152 | tf_op jit(solution)/shard_map/all_to_all | solution.py:155
  284.7 173.1 %all-reduce.3.cloned.1.call-start = ((), (), s32[]{:S(2)}) async-start(), calls=%async_computation.3 | async-start | bytes 3932160 | tf_op jit(solution)/shard_map/psum | solution.py:166
  290.5 12.7 %copy-start.37 = (f32[2048]{0:T(1024)S(1)}, f32[2048]{0:T(1024)}, u32[]{:S(2)}) copy-start(f32[2048]{0:T(1024)} %copy-done.36) | copy-start | bytes 24580
  291.3 13.5 %copy-start.12 = (bf16[2048,256]{1,0:T(8,128)(2,1)S(1)}, bf16[2048,256]{1,0:T(8,128)(2,1)}, u32[]{:S(2)}) copy-start(bf16[2048,256]{1,0:T(8,128)(2,1)} %copy-done.11) | copy-start | bytes 3145732
  (36 other events, 173.0 us)
Sparse Core Ops, SparseCore 0:
  309.5 148.2 all-reduce.2
where the time goes:
time: 482 us; the launch traced here: 472 us
  waiting for transfers between devices  156 us (32%)
  other arithmetic  109 us (23%)
  local copies, waits for them, and re-layouts  82.3 us (17%)
  starting transfers between devices  74.6 us (15%)
  matrix products  35 us (7%)
  between operations  15.3 us (3%)
    psum x1, waiting for transfers between devices, per_device(): lax.psum((in_term, out_term, src_grad, dst_grad, msg_grad), ('grid', 'dom'))  132 us
    gather x4, local copies, waits for them, and re-layouts, per_device(): pre_edge = from_src[edge_src] + from_dst[edge_dst]  35.1 us
    scatter-add x2, other arithmetic, per_device(): jax.ops.segment_sum(grad_pre, edge_dst, num_segments=node_count)  25.2 us
    scatter-add x2, other arithmetic, per_device(): jax.ops.segment_sum(grad_pre, edge_src, num_segments=src_table.shape[0])  24.7 us
    scatter-add x2, other arithmetic, per_device(): gathered = jax.ops.segment_sum(message, edge_dst, num_segments=node_count)  24.5 us
    ppermute x8, starting transfers between devices, passed_along(): return lax.ppermute(shard, axis, pairs)  22.6 us
    gather x2, local copies, waits for them, and re-layouts, per_device(): grad_msg = (grad_state[edge_dst] * edge_scale[:, None]).astype(jnp.bfloat16)  17.2 us
    unnamed x107, local copies, waits for them, and re-layouts  15.5 us
  transfers between devices with their start and end apart: 20, of which 5 were waited for; matrix products, arithmetic and copies ran while one was open for 13% of the time, Pallas kernels for 0%

commit v1 on v0

v1 whole, which is shorter than its diff:
```python
import functools

import jax
import jax.numpy as jnp
from jax import lax
from jax.experimental import pallas as pl
from jax.experimental.pallas import tpu as pltpu
from jax.sharding import PartitionSpec as P

MESH = pl.DeviceIdType.MESH
BF = jnp.bfloat16
F32 = jnp.float32
CH = 256
LANES = 128
TILE = 16


def mm(a, b):
    return lax.dot_general(a, b, (((1,), (0,)), ((), ())), preferred_element_type=F32)


def mt(a, b):
    return lax.dot_general(a, b, (((1,), (1,)), ((), ())), preferred_element_type=F32)


def tm(a, b):
    return lax.dot_general(a, b, (((0,), (0,)), ((), ())), preferred_element_type=F32)


def wide(x):
    return jnp.concatenate([x, x], axis=1)


def hot(equal):
    return jnp.where(equal, 1.0, 0.0).astype(BF)


def step_kernel(
    n_grid, n_dom,
    cols, live, cweight, slot, static, bidx, esrc, edst, elive, eweight,
    enc_in, enc_out, src_proj, dst_proj, msg_proj, cot,
    node_out, gall,
    aux_tx, aux_rx, rx, srow, crow, ccol, ecol,
    so, sr, sot, srt, dd, ddt, bb, bbt, pp, ppt,
    hh, rim, rim_tx, gt_tx, gt_rx,
    eact, edsilu, cemb, pre0, pre1, act0, act1, msg, gm0, gm1, ga1, gp, gs_own, gs_rim, gd, gh,
    acc, g1, g0, ge, gr, ag,
    a2a_send, a2a_recv, aux_send, aux_recv, rim_send, rim_recv, gt_send, gt_recv,
    rs_send, rs_recv, ag_send, ag_recv, own_sem,
):
    n_dev = n_grid * n_dom
    n_node = static.shape[0]
    n_edge = so.shape[0]
    n_col = cols.shape[0]
    n_bnd = bb.shape[0]
    rows_e = n_edge // LANES
    rows_c = n_col // LANES
    g = lax.axis_index("grid")
    o = lax.axis_index("dom")
    me = g * n_dom + o

    def coords(d):
        return (d // n_dom, lax.rem(d, n_dom))

    def others(fn):
        def body(k, carry):
            fn(lax.rem(me + k, n_dev))
            return carry
        lax.fori_loop(1, n_dev, body, 0)

    def loop(n, fn):
        def body(k, carry):
            fn(k)
            return carry
        lax.fori_loop(0, n, body, 0)

    barrier = pltpu.get_barrier_semaphore()
    others(lambda d: pl.semaphore_signal(barrier, inc=1, device_id=coords(d), device_id_type=MESH))

    lane = lax.broadcasted_iota(jnp.int32, (rows_c, LANES), 1)
    quarter = lax.rem(me, 4)
    slot_f = slot[...].astype(F32)
    scale_f = cweight[...] * live[...].astype(F32)
    for j in range(8):
        to_slot = lax.rem((quarter - j) * 16 + 2 * LANES, LANES)
        to_scale = lax.rem((quarter - j) * 16 + 64 + 2 * LANES, LANES)
        a = pltpu.roll(slot_f, to_slot, axis=1)
        b = pltpu.roll(scale_f, to_scale, axis=1)
        row = jnp.where(lane // 16 == quarter, a, jnp.where(lane // 16 == quarter + 4, b, 0.0))
        aux_tx[pl.ds(j, rows_c, stride=8), :] = row

    pl.semaphore_wait(barrier, n_dev - 1)

    def send_cols(d):
        pltpu.make_async_remote_copy(
            src_ref=cols.at[pl.ds(pl.multiple_of(d * TILE, TILE), TILE), :],
            dst_ref=rx.at[pl.ds(pl.multiple_of(me * TILE, TILE), TILE), :],
            send_sem=a2a_send, recv_sem=a2a_recv, device_id=coords(d), device_id_type=MESH,
        ).start()
        pltpu.make_async_remote_copy(
            src_ref=aux_tx.at[d], dst_ref=aux_rx.at[me],
            send_sem=aux_send, recv_sem=aux_recv, device_id=coords(d), device_id_type=MESH,
        ).start()

    others(send_cols)
    mine = pl.ds(pl.multiple_of(me * TILE, TILE), TILE)
    rx[mine, :] = cols[mine, :]
    aux_rx[me] = aux_tx[me]

    here = (g > 0, g < n_grid - 1, o > 0, o < n_dom - 1)
    near = ((g - 1, o), (g + 1, o), (g, o - 1), (g, o + 1))
    flip = (1, 0, 3, 2)
    for r in range(4):
        @pl.when(jnp.logical_not(here[r]))
        def _():
            for l in range(2):
                rim[l, r] = jnp.zeros((n_bnd, 256), BF)
                gt_rx[l, flip[r]] = jnp.zeros((n_bnd, 256), BF)

    lane_i = lax.broadcasted_iota(jnp.int32, (LANES, LANES), 1)
    sub_i = lax.broadcasted_iota(jnp.int32, (LANES, LANES), 0)

    def across(row):
        full = jnp.broadcast_to(row, (LANES, LANES))
        return full, jnp.transpose(full)

    def build_edges(b):
        at = pl.ds(pl.multiple_of(b * LANES, LANES), LANES)
        full, down = across(edst[pl.ds(b, 1), :])
        for c in range(n_node // LANES):
            part = slice(c * LANES, (c + 1) * LANES)
            dd[at, part] = hot(down == lane_i + c * LANES)
            ddt[part, at] = hot(full == sub_i + c * LANES)
        scale = eweight[pl.ds(b, 1), :] * elive[pl.ds(b, 1), :].astype(F32)
        ecol[at, :] = across(scale)[1]
        full, down = across(esrc[pl.ds(b, 1), :])
        for c in range(n_node // LANES):
            part = slice(c * LANES, (c + 1) * LANES)
            so[at, part] = hot(down == lane_i + c * LANES)
            sot[part, at] = hot(full == sub_i + c * LANES)
        for c in range(4 * n_bnd // LANES):
            part = slice(c * LANES, (c + 1) * LANES)
            sr[at, part] = hot(down == lane_i + (n_node + c * LANES))
            srt[part, at] = hot(full == sub_i + (n_node + c * LANES))

    loop(rows_e, build_edges)

    def build_bound(b):
        at = pl.ds(pl.multiple_of(b * LANES, LANES), LANES)
        full, down = across(bidx[pl.ds(b, 1), :])
        for c in range(n_node // LANES):
            part = slice(c * LANES, (c + 1) * LANES)
            bb[at, part] = hot(down == lane_i + c * LANES)
            bbt[part, at] = hot(full == sub_i + c * LANES)

    loop(n_bnd // LANES, build_bound)

    def chunk(c):
        return pl.ds(pl.multiple_of(c * CH, CH), CH)

    def back_last(c):
        at = chunk(c)
        rows = (mm(dd[at, :], cot[...]) * wide(ecol[at, :])).astype(BF)
        gm1[at, :] = rows
        ga1[at, :] = mt(rows, msg_proj[1])

    loop(n_edge // CH, back_last)

    got = pl.ds(0, (n_dev - 1) * TILE)
    cols_done = pltpu.make_async_remote_copy(
        src_ref=rx.at[got, :], dst_ref=rx.at[got, :], send_sem=a2a_send, recv_sem=a2a_recv,
        device_id=(g, o), device_id_type=MESH)
    got_aux = pl.ds(0, n_dev - 1)
    aux_done = pltpu.make_async_remote_copy(
        src_ref=aux_rx.at[got_aux], dst_ref=aux_rx.at[got_aux], send_sem=aux_send, recv_sem=aux_recv,
        device_id=(g, o), device_id_type=MESH)
    cols_done.wait_recv()
    aux_done.wait_recv()
    parts = aux_rx[...].reshape(rows_c, 8, LANES)
    low = jnp.sum(parts[:, 0:4, :], axis=1)
    high = jnp.sum(parts[:, 4:8, :], axis=1)
    srow[...] = jnp.where(lane < 64, low, pltpu.roll(high, 64, axis=1))
    crow[...] = jnp.where(lane < 64, pltpu.roll(low, 64, axis=1), high)

    lane_f = lane_i.astype(F32)
    sub_f = sub_i.astype(F32)

    def build_pool(b):
        at = pl.ds(pl.multiple_of(b * LANES, LANES), LANES)
        full, down = across(srow[pl.ds(b, 1), :])
        for c in range(n_node // LANES):
            part = slice(c * LANES, (c + 1) * LANES)
            pp[at, part] = hot(down == lane_f + float(c * LANES))
            ppt[part, at] = hot(full == sub_f + float(c * LANES))
        ccol[at, :] = across(crow[pl.ds(b, 1), :])[1]

    loop(rows_c, build_pool)

    def sigmoid(v):
        return 0.5 * jnp.tanh(0.5 * v) + 0.5

    def encode(c):
        at = chunk(c)
        v = mm(rx[at, :], enc_in[...])
        s = sigmoid(v)
        a = (v * s).astype(BF)
        eact[at, :] = a
        edsilu[at, :] = s * (1.0 + v * (1.0 - s))
        cemb[at, :] = (mm(a, enc_out[...]) * wide(ccol[at, :])).astype(BF)

    loop(n_col // CH, encode)

    def pool(c):
        at = chunk(c)
        hh[0, at, :] = (static[at, :].astype(F32) + mm(ppt[at, :], cemb[...])).astype(BF)

    loop(n_node // CH, pool)

    def fwd_copy(l, r):
        return pltpu.make_async_remote_copy(
            src_ref=rim_tx.at[l], dst_ref=rim.at[l, r], send_sem=rim_send.at[l, r],
            recv_sem=rim_recv.at[l, r], device_id=near[flip[r]], device_id_type=MESH)

    def back_copy(l, r):
        return pltpu.make_async_remote_copy(
            src_ref=gt_tx.at[l, r], dst_ref=gt_rx.at[l, r], send_sem=gt_send.at[l, r],
            recv_sem=gt_recv.at[l, r], device_id=near[r], device_id_type=MESH)

    def send_rims(l):
        rim_tx[l] = mm(bb[...], hh[l]).astype(BF)
        for r in (2, 3, 0, 1):
            @pl.when(here[flip[r]])
            def _():
                fwd_copy(l, r).start()

    def wait_rims(l):
        for r in range(4):
            @pl.when(here[r])
            def _():
                fwd_copy(l, r).wait_recv()

    def layer_own(l, pre):
        def body(c):
            at = chunk(c)
            h = hh[l]
            xo = mm(so[at, :], h).astype(BF)
            xd = mm(dd[at, :], h).astype(BF)
            pre[at, :] = mm(xo, src_proj[l]) + mm(xd, dst_proj[l])
        loop(n_edge // CH, body)

    def layer_rest(l, pre, act):
        def body(c):
            at = chunk(c)
            xr = mm(sr[at, :], rim[l].reshape(4 * n_bnd, 256)).astype(BF)
            v = pre[at, :] + mm(xr, src_proj[l])
            s = sigmoid(v)
            a = (v * s).astype(BF)
            act[at, :] = a
            slope = s * (1.0 + v * (1.0 - s))
            if l == 0:
                pre[at, :] = slope
            else:
                gp[at, :] = (ga1[at, :] * slope).astype(BF)
            msg[at, :] = (mm(a, msg_proj[l]) * wide(ecol[at, :])).astype(BF)
        loop(n_edge // CH, body)

    def gather_messages(l):
        def body(c):
            at = chunk(c)
            rows = (hh[l, at, :].astype(F32) + mm(ddt[at, :], msg[...])).astype(BF)
            if l == 0:
                hh[1, at, :] = rows
            else:
                node_out[at, :] = rows
        loop(n_node // CH, body)

    send_rims(0)
    layer_own(0, pre0)
    wait_rims(0)
    layer_rest(0, pre0, act0)
    gather_messages(0)
    send_rims(1)
    layer_own(1, pre1)
    wait_rims(1)
    layer_rest(1, pre1, act1)

    def back_rims(l):
        for r in (2, 3, 0, 1):
            rows = mm(srt[r * n_bnd:(r + 1) * n_bnd, :], gp[...]).astype(BF)
            gs_rim[r] = rows
            gt_tx[l, r] = mt(rows, src_proj[l]).astype(BF)

            @pl.when(here[r])
            def _():
                back_copy(l, r).start()

    def back_own(l):
        def body(c):
            at = chunk(c)
            s_rows = mm(sot[at, :], gp[...]).astype(BF)
            d_rows = mm(ddt[at, :], gp[...]).astype(BF)
            gs_own[at, :] = s_rows
            gd[at, :] = d_rows
            before = cot[at, :].astype(F32) if l == 1 else gh[at, :]
            gh[at, :] = before + mt(s_rows, src_proj[l]) + mt(d_rows, dst_proj[l])
        loop(n_node // CH, body)

    def layer_weights(l, act, gm, out):
        total = tm(hh[l], gs_own[...])
        for r in range(4):
            total = total + tm(rim[l, r], gs_rim[r])
        out[0:256, :] = total.astype(BF)
        out[256:512, :] = tm(hh[l], gd[...]).astype(BF)
        acc[...] = jnp.zeros_like(acc)

        def body(c):
            at = chunk(c)
            acc[...] += tm(act[at, :], gm[at, :])
        loop(n_edge // CH, body)
        out[512:768, :] = acc[...].astype(BF)

    def add_rims(l):
        for r in range(4):
            @pl.when(here[flip[r]])
            def _():
                back_copy(l, r).wait_recv()

        def body(c):
            at = chunk(c)
            total = gh[at, :]
            for r in range(4):
                total = total + mm(bbt[at, :], gt_rx[l, r])
            gh[at, :] = total
        loop(n_node // CH, body)

    rounds = ((96, 0, 0), (96, 96, 96), (48, 64, 192))

    def tile_of(k, d):
        return lax.rem(d - rounds[k][1] + n_dev, n_dev)

    def tile_at(ref, t):
        return ref.at[pl.ds(pl.multiple_of((t // 2) * TILE, TILE), TILE),
                      pl.ds(pl.multiple_of(lax.rem(t, 2) * LANES, LANES), LANES)]

    def rs_copy(k, ref, d):
        return pltpu.make_async_remote_copy(
            src_ref=tile_at(ref, tile_of(k, d)), dst_ref=gr.at[k, me], send_sem=rs_send.at[k],
            recv_sem=rs_recv.at[k], device_id=coords(d), device_id_type=MESH)

    def scatter_start(k, ref):
        count = rounds[k][0]

        def one(d):
            @pl.when(tile_of(k, d) < count)
            def _():
                rs_copy(k, ref, d).start()
        others(one)

        @pl.when(tile_of(k, me) < count)
        def _():
            t = tile_of(k, me)
            gr[k, me] = ref[pl.ds(pl.multiple_of((t // 2) * TILE, TILE), TILE),
                            pl.ds(pl.multiple_of(lax.rem(t, 2) * LANES, LANES), LANES)]

    def span_wait(k, n, sems, what):
        at = pl.ds(0, n)
        copy = pltpu.make_async_remote_copy(
            src_ref=gr.at[k, at], dst_ref=gr.at[k, at], send_sem=sems.at[k], recv_sem=sems.at[k],
            device_id=(g, o), device_id_type=MESH)
        if what == "recv":
            copy.wait_recv()
        else:
            copy.wait_send()

    def ag_copy(k, d):
        return pltpu.make_async_remote_copy(
            src_ref=ag.at[k], dst_ref=gall.at[rounds[k][2] + tile_of(k, me)], send_sem=ag_send.at[k],
            recv_sem=ag_recv.at[k], device_id=coords(d), device_id_type=MESH)

    def own_copy(k):
        return pltpu.make_async_copy(ag.at[k], gall.at[rounds[k][2] + tile_of(k, me)], own_sem.at[k])

    def gather_start(k):
        @pl.when(tile_of(k, me) < rounds[k][0])
        def _():
            span_wait(k, n_dev - 1, rs_recv, "recv")

            def body(s, total):
                for i in range(8):
                    total = total + gr[k, s * 8 + i].astype(F32)
                return total
            total = lax.fori_loop(0, n_dev // 8, body, jnp.zeros((TILE, LANES), F32))
            ag[k] = total.astype(BF)
            own_copy(k).start()
            others(lambda d: ag_copy(k, d).start())

    def finish(k):
        count = rounds[k][0]

        @pl.when(tile_of(k, me) < count)
        def _():
            own_copy(k).wait()
            span_wait(k, count - 1, rs_send, "send")
            span_wait(k, n_dev - 1, ag_send, "send")
            at = pl.ds(0, count - 1)
            pltpu.make_async_remote_copy(
                src_ref=gall.at[at], dst_ref=gall.at[at], send_sem=ag_send.at[k],
                recv_sem=ag_recv.at[k], device_id=(g, o), device_id_type=MESH).wait_recv()

        @pl.when(tile_of(k, me) >= count)
        def _():
            span_wait(k, count, rs_send, "send")
            at = pl.ds(0, count)
            pltpu.make_async_remote_copy(
                src_ref=gall.at[at], dst_ref=gall.at[at], send_sem=ag_send.at[k],
                recv_sem=ag_recv.at[k], device_id=(g, o), device_id_type=MESH).wait_recv()

    back_rims(1)
    back_own(1)
    layer_weights(1, act1, gm1, g1)
    scatter_start(0, g1)
    gather_messages(1)
    add_rims(1)

    def back_first(c):
        at = chunk(c)
        rows = (mm(dd[at, :], gh[...].astype(BF)) * wide(ecol[at, :])).astype(BF)
        gm0[at, :] = rows
        gp[at, :] = (mt(rows, msg_proj[0]) * pre0[at, :]).astype(BF)

    loop(n_edge // CH, back_first)
    back_rims(0)
    back_own(0)
    layer_weights(0, act0, gm0, g0)
    scatter_start(1, g0)
    gather_start(0)
    add_rims(0)

    ge[0:256, :] = jnp.zeros((256, 256), BF)
    acc[...] = jnp.zeros_like(acc)

    def encode_out(c):
        at = chunk(c)
        rows = (mm(pp[at, :], gh[...].astype(BF)) * wide(ccol[at, :])).astype(BF)
        acc[...] += tm(eact[at, :], rows)
        cemb[at, :] = (mt(rows, enc_out[...]) * edsilu[at, :]).astype(BF)

    loop(n_col // CH, encode_out)
    ge[0:256, :] = acc[...].astype(BF)
    acc[...] = jnp.zeros_like(acc)

    def encode_in(c):
        at = chunk(c)
        acc[0:128, :] += tm(rx[at, :], cemb[at, :])

    loop(n_col // CH, encode_in)
    ge[256:384, :] = acc[0:128, :].astype(BF)
    scatter_start(2, ge)
    gather_start(1)
    gather_start(2)

    cols_done.wait_send()
    aux_done.wait_send()
    for l in range(2):
        for r in range(4):
            @pl.when(here[flip[r]])
            def _():
                fwd_copy(l, r).wait_send()

            @pl.when(here[r])
            def _():
                back_copy(l, r).wait_send()
    for k in range(3):
        finish(k)


def finish_kernel(gall, node_in, enc_in_g, enc_out_g, src_g, dst_g, msg_g, node_out):
    node_out[...] = node_in[...]
    layer_refs = (src_g, dst_g, msg_g)

    def put(first, count, store):
        for t in range(count):
            rb, half = t // 2, t % 2
            rows = slice(rb * TILE, (rb + 1) * TILE)
            store(rows, slice(half * LANES, (half + 1) * LANES), gall[first + t].astype(F32))

    for layer, first in ((1, 0), (0, 96)):
        for m in range(3):
            def store(rows, lanes, v, ref=layer_refs[m], layer=layer):
                ref[layer, rows, lanes] = v
            put(first + 32 * m, 32, store)

    def store_out(rows, lanes, v):
        enc_out_g[rows, lanes] = v

    def store_in(rows, lanes, v):
        enc_in_g[rows, lanes] = v

    put(192, 32, store_out)
    put(224, 16, store_in)


def per_device(n_grid, n_dom, columns, column_live, col_weight, col_slot, node_static, boundary_idx,
               edge_src, edge_dst, edge_live, edge_weight, enc_in, enc_out, src_proj, dst_proj, msg_proj,
               node_cotangent):
    n_dev = n_grid * n_dom
    n_col = columns.shape[0]
    n_edge = edge_src.shape[0]
    n_node, width = node_static.shape
    n_bnd = boundary_idx.shape[0]
    rows = lambda x: x.reshape(-1, LANES)
    vm = lambda *shape: pltpu.VMEM(shape, BF)
    vf = lambda *shape: pltpu.VMEM(shape, F32)
    dma = pltpu.SemaphoreType.DMA
    scratch = [
        vf(n_dev, LANES), vf(n_dev, LANES), vm(n_col, columns.shape[1]), vf(n_col // LANES, LANES),
        vf(n_col // LANES, LANES), vf(n_col, LANES), vf(n_edge, LANES),
        vm(n_edge, n_node), vm(n_edge, 4 * n_bnd), vm(n_node, n_edge), vm(4 * n_bnd, n_edge),
        vm(n_edge, n_node), vm(n_node, n_edge), vm(n_bnd, n_node), vm(n_node, n_bnd),
        vm(n_col, n_node), vm(n_node, n_col),
        vm(2, n_node, width), vm(2, 4, n_bnd, width), vm(2, n_bnd, width), vm(2, 4, n_bnd, width),
        vm(2, 4, n_bnd, width),
        vm(n_col, width), vf(n_col, width), vm(n_col, width), vf(n_edge, width), vf(n_edge, width),
        vm(n_edge, width), vm(n_edge, width), vm(n_edge, width), vm(n_edge, width), vm(n_edge, width),
        vf(n_edge, width), vm(n_edge, width), vm(n_node, width), vm(4, n_bnd, width), vm(n_node, width),
        vf(n_node, width),
        vf(width, width), vm(768, width), vm(768, width), vm(384, width), vm(3, n_dev, TILE, LANES),
        vm(3, TILE, LANES),
        dma(()), dma(()), dma(()), dma(()), dma((2, 4)), dma((2, 4)), dma((2, 4)), dma((2, 4)),
        dma((3,)), dma((3,)), dma((3,)), dma((3,)), dma((3,)),
    ]
    in_vmem = pl.BlockSpec(memory_space=pltpu.VMEM)
    node_out, gall = pl.pallas_call(
        functools.partial(step_kernel, n_grid, n_dom),
        out_shape=(jax.ShapeDtypeStruct((n_node, width), BF), jax.ShapeDtypeStruct((240, TILE, LANES), BF)),
        in_specs=[in_vmem] * 16,
        out_specs=(in_vmem, pl.BlockSpec(memory_space=pl.ANY)),
        scratch_shapes=scratch,
        compiler_params=pltpu.CompilerParams(
            collective_id=0, has_side_effects=True, vmem_limit_bytes=62 * 1024 * 1024),
    )(columns, rows(column_live), rows(col_weight), rows(col_slot), node_static, rows(boundary_idx),
      rows(edge_src), rows(edge_dst), rows(edge_live), rows(edge_weight), enc_in, enc_out, src_proj,
      dst_proj, msg_proj, node_cotangent)
    mat = jax.ShapeDtypeStruct((width, width), F32)
    pair = jax.ShapeDtypeStruct((2, width, width), F32)
    enc_in_g, enc_out_g, src_g, dst_g, msg_g, node_final = pl.pallas_call(
        finish_kernel,
        out_shape=(jax.ShapeDtypeStruct(enc_in.shape, F32), mat, pair, pair, pair,
                   jax.ShapeDtypeStruct((n_node, width), BF)),
        in_specs=[in_vmem] * 2,
        out_specs=(in_vmem,) * 6,
    )(gall, node_out)
    return (node_final, enc_in_g, enc_out_g, src_g, dst_g, msg_g)


def solution(mesh):
    n_grid, n_dom = mesh.shape["grid"], mesh.shape["dom"]
    both = P(("grid", "dom"))
    rows = P(("grid", "dom"), None)
    placed = (rows, both, both, both, rows, both, both, both, both, both, P(), P(), P(), P(), P(), rows)
    return jax.shard_map(
        functools.partial(per_device, n_grid, n_dom),
        mesh=mesh,
        in_specs=placed,
        out_specs=(rows, P(), P(), P(), P(), P()),
        check_vma=False,
    )
```

time: 482 us -> 115 us (0.24); the launches traced: 472 us -> 115 us
  waiting for transfers between devices: 156 us -> 0 us
  Pallas kernels: 0 us -> 114 us
  other arithmetic: 109 us -> 0 us
  local copies, waits for them, and re-layouts: 82.3 us -> 0 us
  starting transfers between devices: 74.6 us -> 0 us
  matrix products: 35 us -> 0 us
  between operations: 15.3 us -> 0.65 us
    psum x1 -> x0, waiting for transfers between devices: 132 us -> none  [per_device(): lax.psum((in_term, out_term, src_grad, dst_grad, msg_grad), ('grid', 'dom'))]
    pallas_call x0 -> x2, Pallas kernels: none -> 114 us  [the longest x1 111 us: per_device(): pl.pallas_call(functools.partial(step_kernel, n_grid, n_dom), out_shape=(...]
    scatter-add x9 -> x0, other arithmetic: 93.4 us -> none  [the longest x2 25.2 us: per_device(): jax.ops.segment_sum(grad_pre, edge_dst, num_segments=node_count)]
    gather x9 -> x0, local copies, waits for them, and re-layouts: 63.9 us -> none  [the longest x4 35.1 us: per_device(): pre_edge = from_src[edge_src] + from_dst[edge_dst]]
    ppermute x16 -> x0, starting transfers between devices: 44.8 us -> none  [the longest x8 22.6 us: passed_along(): return lax.ppermute(shard, axis, pairs)]
    dot_general x22 -> x0, matrix products: 35 us -> none  [the longest x8 13.9 us: outer_sum(): lax.dot_general(left_side, right_side, (((0,), (0,)), ((), ())), preferre...]
    all_to_all x3 -> x0, starting transfers between devices: 29.5 us -> none  [the longest x1 11.8 us: per_device(): lax.all_to_all(back_rows, ('grid', 'dom'), split_axis=0, concat_axis=0, t...]
    all_to_all x3 -> x0, waiting for transfers between devices: 22.3 us -> none  [the longest x1 10.8 us: per_device(): lax.all_to_all(back_rows, ('grid', 'dom'), split_axis=0, concat_axis=0, t...]
  transfers between devices with their start and end apart: 20 -> 0, of which waited for: 5 -> 0; matrix products, arithmetic and copies ran while one was open for 13% -> 0% of each run, Pallas kernels for 0% -> 0%
where the time goes in v1:
time: 115 us
  Pallas kernels  114 us (99%)
    pallas_call x1, Pallas kernels, per_device(): pl.pallas_call(functools.partial(step_kernel, n_grid, n_dom), out_shape=(...  111 us
    pallas_call x1, Pallas kernels, per_device(): pl.pallas_call(finish_kernel, out_shape=(jax.ShapeDtypeStruct(enc_in.shap...  2.63 us

profile of v1, /device:TPU:1, one launch (start us, length us, event | category | flops | bytes accessed | tf_op | source)
XLA Modules:
  0.0 114.8 jit_solution(7282825811653687996)
XLA Ops:
  0.6 111.5 %shard_map.199 = (bf16[512,256]{1,0:T(8,128)(2,1)}, bf16[240,16,128]{2,1,0:T(8,128)(2,1)}) custom-call(bf16[2048,128]{1,0:T(8,128)(2,1)} %cols.1, s32[16,128]{1,0:T(8,128)} %bitcast.8, f32[16,128]{1,0:T(8,128)} %bitcast.9, s32[16,128]{1,0:T(8,128)} %bitcast.10, bf16[512,256]{1,0:T(8,128)(2,1)} %static.1, s32[2,128]{1,0:T(2,128)} %bitcast.15, ...), custom_call_target="tpu_custom_call" | custom-call | tf_op jit(solution)/shard_map/pallas_call | solution.py:533
  112.1 2.6 %shard_map.200 = (f32[128,256]{1,0:T(8,128)}, f32[256,256]{1,0:T(8,128)}, f32[2,256,256]{2,1,0:T(8,128)}, f32[2,256,256]{2,1,0:T(8,128)}, f32[2,256,256]{2,1,0:T(8,128)}, /*index=5*/bf16[512,256]{1,0:T(8,128)(2,1)}) custom-call(bf16[240,16,128]{2,1,0:T(8,128)(2,1)} %get-tuple-element.14.gall, bf16[512,256]{1,0:T(8,128)(2,1)} %get-tuple-element.15.node_in), custom_call_target="tpu_custom_call" | custom-call | tf_op jit(solution)/shard_map/pallas_call | solution.py:546

commit v2 on v1

--- a/solution.py
+++ b/solution.py
@@ -10,7 +10,7 @@
 MESH = pl.DeviceIdType.MESH
 BF = jnp.bfloat16
 F32 = jnp.float32
-CH = 256
+CH = 512
 LANES = 128
 TILE = 16
 
@@ -37,17 +37,27 @@
 
 def step_kernel(
     n_grid, n_dom,
-    cols, live, cweight, slot, static, bidx, esrc, edst, elive, eweight,
-    enc_in, enc_out, src_proj, dst_proj, msg_proj, cot,
-    node_out, gall,
-    aux_tx, aux_rx, rx, srow, crow, ccol, ecol,
+    n_in, *refs,
+):
+    inputs = refs[:n_in]
+    node_out, gall = refs[n_in:n_in + 2]
+    copies = refs[n_in + 2:2 * n_in + 2]
+    step_body(n_grid, n_dom, inputs, copies, node_out, gall, *refs[2 * n_in + 2:])
+
+
+def step_body(
+    n_grid, n_dom, inputs, copies, node_out, gall,
+    in_sem, round_sem, aux_tx, aux_rx, rx, srow, crow, ccol, ecol,
     so, sr, sot, srt, dd, ddt, bb, bbt, pp, ppt,
     hh, rim, rim_tx, gt_tx, gt_rx,
     eact, edsilu, cemb, pre0, pre1, act0, act1, msg, gm0, gm1, ga1, gp, gs_own, gs_rim, gd, gh,
-    acc, g1, g0, ge, gr, ag,
+    acc, g1, g0, ge, px1, px0, pxe, tx1, tx0, txe, gr, ag,
+    pair_send, pair_recv,
     a2a_send, a2a_recv, aux_send, aux_recv, rim_send, rim_recv, gt_send, gt_recv,
     rs_send, rs_recv, ag_send, ag_recv, own_sem,
 ):
+    (cols, live, cweight, slot, static, bidx, esrc, edst, elive, eweight,
+     enc_in, enc_out, src_proj, dst_proj, msg_proj, cot) = copies
     n_dev = n_grid * n_dom
     n_node = static.shape[0]
     n_edge = so.shape[0]
@@ -59,14 +69,28 @@
     o = lax.axis_index("dom")
     me = g * n_dom + o
 
-    def coords(d):
-        return (d // n_dom, lax.rem(d, n_dom))
-
-    def others(fn):
-        def body(k, carry):
-            fn(lax.rem(me + k, n_dev))
+    core = lax.rem(g, 2)
+    z = g // 2
+    n_z, n_y, n_x = n_grid // 2, n_dom // 4, 4
+    y, x = o // n_x, lax.rem(o, n_x)
+    chip = z * n_dom + o
+    n_chip = n_dev // 2
+
+    def others(fn, cores=(1, 0)):
+        def some(i, skip):
+            to_z = lax.rem(z + (n_z - 1 - i // n_y), n_z)
+            to_y = lax.rem(y + (n_y - 1 - lax.rem(i, n_y)), n_y)
+            for dx in (2, 1, 3, 0):
+                to_o = to_y * n_x + lax.rem(x + dx, n_x)
+                for dc in cores:
+                    if not (skip and dx == 0 and dc == 0):
+                        fn(to_z * 2 + (1 - core if dc else core), to_o)
+
+        def body(i, carry):
+            some(i, False)
             return carry
-        lax.fori_loop(1, n_dev, body, 0)
+        lax.fori_loop(0, n_z * n_y - 1, body, 0)
+        some(n_z * n_y - 1, True)
 
     def loop(n, fn):
         def body(k, carry):
@@ -74,8 +98,26 @@
             return carry
         lax.fori_loop(0, n, body, 0)
 
+    def load(i):
+        return pltpu.make_async_copy(inputs[i], copies[i], in_sem.at[i])
+
     barrier = pltpu.get_barrier_semaphore()
-    others(lambda d: pl.semaphore_signal(barrier, inc=1, device_id=coords(d), device_id_type=MESH))
+
+    def column(fn):
+        for k in range(1, n_grid):
+            fn((lax.rem(g + k, n_grid), o))
+
+    def greet(sem, to):
+        pl.semaphore_signal(sem, inc=1, device_id=to, device_id_type=MESH)
+
+    for k in range(1, n_dom):
+        greet(barrier, (g, lax.rem(o + k, n_dom)))
+    column(lambda to: greet(barrier, to))
+    order = (0, 1, 2, 3, 6, 7, 8, 9, 5, 15, 14, 10, 11, 4, 12, 13)
+    for i in order:
+        load(i).start()
+    for i in order[:4]:
+        load(i).wait()
 
     lane = lax.broadcasted_iota(jnp.int32, (rows_c, LANES), 1)
     quarter = lax.rem(me, 4)
@@ -89,20 +131,29 @@
         row = jnp.where(lane // 16 == quarter, a, jnp.where(lane // 16 == quarter + 4, b, 0.0))
         aux_tx[pl.ds(j, rows_c, stride=8), :] = row
 
-    pl.semaphore_wait(barrier, n_dev - 1)
-
-    def send_cols(d):
+    pl.semaphore_wait(barrier, n_dom + n_grid - 2)
+    column(lambda to: greet(round_sem, to))
+    pl.semaphore_wait(round_sem, n_grid - 1)
+
+    def send_aux(to_g, to_o):
+        d = to_g * n_dom + to_o
+        pltpu.make_async_remote_copy(
+            src_ref=aux_tx.at[d], dst_ref=aux_rx.at[me],
+            send_sem=aux_send, recv_sem=aux_recv, device_id=(to_g, to_o), device_id_type=MESH,
+        ).start()
+
+    def send_cols(to_g, to_o):
+        d = to_g * n_dom + to_o
         pltpu.make_async_remote_copy(
             src_ref=cols.at[pl.ds(pl.multiple_of(d * TILE, TILE), TILE), :],
             dst_ref=rx.at[pl.ds(pl.multiple_of(me * TILE, TILE), TILE), :],
-            send_sem=a2a_send, recv_sem=a2a_recv, device_id=coords(d), device_id_type=MESH,
+            send_sem=a2a_send, recv_sem=a2a_recv, device_id=(to_g, to_o), device_id_type=MESH,
         ).start()
-        pltpu.make_async_remote_copy(
-            src_ref=aux_tx.at[d], dst_ref=aux_rx.at[me],
-            send_sem=aux_send, recv_sem=aux_recv, device_id=coords(d), device_id_type=MESH,
-        ).start()
-
+
+    others(send_aux)
     others(send_cols)
+    for i in order[4:]:
+        load(i).wait()
     mine = pl.ds(pl.multiple_of(me * TILE, TILE), TILE)
     rx[mine, :] = cols[mine, :]
     aux_rx[me] = aux_tx[me]
@@ -174,7 +225,6 @@
     aux_done = pltpu.make_async_remote_copy(
         src_ref=aux_rx.at[got_aux], dst_ref=aux_rx.at[got_aux], send_sem=aux_send, recv_sem=aux_recv,
         device_id=(g, o), device_id_type=MESH)
-    cols_done.wait_recv()
     aux_done.wait_recv()
     parts = aux_rx[...].reshape(rows_c, 8, LANES)
     low = jnp.sum(parts[:, 0:4, :], axis=1)
@@ -195,6 +245,7 @@
         ccol[at, :] = across(crow[pl.ds(b, 1), :])[1]
 
     loop(rows_c, build_pool)
+    cols_done.wait_recv()
 
     def sigmoid(v):
         return 0.5 * jnp.tanh(0.5 * v) + 0.5
@@ -305,19 +356,24 @@
             gh[at, :] = before + mt(s_rows, src_proj[l]) + mt(d_rows, dst_proj[l])
         loop(n_node // CH, body)
 
+    def halves(out, first, value):
+        rows = slice(first, first + value.shape[0])
+        out[0, rows, :] = value[:, 0:LANES]
+        out[1, rows, :] = value[:, LANES:]
+
     def layer_weights(l, act, gm, out):
         total = tm(hh[l], gs_own[...])
         for r in range(4):
             total = total + tm(rim[l, r], gs_rim[r])
-        out[0:256, :] = total.astype(BF)
-        out[256:512, :] = tm(hh[l], gd[...]).astype(BF)
+        halves(out, 0, total)
+        halves(out, 256, tm(hh[l], gd[...]))
         acc[...] = jnp.zeros_like(acc)
 
         def body(c):
             at = chunk(c)
             acc[...] += tm(act[at, :], gm[at, :])
         loop(n_edge // CH, body)
-        out[512:768, :] = acc[...].astype(BF)
+        halves(out, 512, acc[...])
 
     def add_rims(l):
         for r in range(4):
@@ -333,93 +389,102 @@
             gh[at, :] = total
         loop(n_node // CH, body)
 
-    rounds = ((96, 0, 0), (96, 96, 96), (48, 64, 192))
-
-    def tile_of(k, d):
-        return lax.rem(d - rounds[k][1] + n_dev, n_dev)
-
-    def tile_at(ref, t):
-        return ref.at[pl.ds(pl.multiple_of((t // 2) * TILE, TILE), TILE),
-                      pl.ds(pl.multiple_of(lax.rem(t, 2) * LANES, LANES), LANES)]
-
-    def rs_copy(k, ref, d):
+    rounds = ((48, 0, 0), (48, 48, 48), (24, 32, 96))
+    parts_of = ((g1, px1, tx1), (g0, px0, tx0), (ge, pxe, txe))
+
+    def tile_of(k, q):
+        return lax.rem(q - rounds[k][1] + n_chip, n_chip)
+
+    def pair_copy(k):
+        mine, theirs, _ = parts_of[k]
         return pltpu.make_async_remote_copy(
-            src_ref=tile_at(ref, tile_of(k, d)), dst_ref=gr.at[k, me], send_sem=rs_send.at[k],
-            recv_sem=rs_recv.at[k], device_id=coords(d), device_id_type=MESH)
-
-    def scatter_start(k, ref):
+            src_ref=mine.at[1 - core], dst_ref=theirs, send_sem=pair_send.at[k],
+            recv_sem=pair_recv.at[k], device_id=(g + 1 - 2 * core, o), device_id_type=MESH)
+
+    def rows_of(t):
+        return pl.ds(pl.multiple_of(t * TILE, TILE), TILE)
+
+    def scatter_start(k):
         count = rounds[k][0]
-
-        def one(d):
-            @pl.when(tile_of(k, d) < count)
+        mine, theirs, out = parts_of[k]
+        pair_copy(k).wait_recv()
+
+        def add(c):
+            at = pl.ds(pl.multiple_of(c * LANES, LANES), LANES)
+            out[at, :] = (mine[core, at, :] + theirs[at, :]).astype(BF)
+        loop(out.shape[0] // LANES, add)
+
+        def one(to_g, to_o):
+            t = tile_of(k, (to_g // 2) * n_dom + to_o)
+
+            @pl.when(t < count)
             def _():
-                rs_copy(k, ref, d).start()
-        others(one)
-
-        @pl.when(tile_of(k, me) < count)
+                pltpu.make_async_remote_copy(
+                    src_ref=out.at[rows_of(t), :], dst_ref=gr.at[k, chip], send_sem=rs_send.at[k],
+                    recv_sem=rs_recv.at[k], device_id=(to_g, to_o), device_id_type=MESH).start()
+        others(one, cores=(0,))
+
+        @pl.when(tile_of(k, chip) < count)
         def _():
-            t = tile_of(k, me)
-            gr[k, me] = ref[pl.ds(pl.multiple_of((t // 2) * TILE, TILE), TILE),
-                            pl.ds(pl.multiple_of(lax.rem(t, 2) * LANES, LANES), LANES)]
-
-    def span_wait(k, n, sems, what):
+            gr[k, chip] = out[rows_of(tile_of(k, chip)), :]
+
+    def span_wait(ref, n, sem, what):
         at = pl.ds(0, n)
         copy = pltpu.make_async_remote_copy(
-            src_ref=gr.at[k, at], dst_ref=gr.at[k, at], send_sem=sems.at[k], recv_sem=sems.at[k],
+            src_ref=ref.at[at], dst_ref=ref.at[at], send_sem=sem, recv_sem=sem,
             device_id=(g, o), device_id_type=MESH)
         if what == "recv":
             copy.wait_recv()
         else:
             copy.wait_send()
 
-    def ag_copy(k, d):
-        return pltpu.make_async_remote_copy(
-            src_ref=ag.at[k], dst_ref=gall.at[rounds[k][2] + tile_of(k, me)], send_sem=ag_send.at[k],
-            recv_sem=ag_recv.at[k], device_id=coords(d), device_id_type=MESH)
+    def place(k):
+        return gall.at[2 * (rounds[k][2] + tile_of(k, chip)) + core]
 
     def own_copy(k):
-        return pltpu.make_async_copy(ag.at[k], gall.at[rounds[k][2] + tile_of(k, me)], own_sem.at[k])
+        return pltpu.make_async_copy(ag.at[k], place(k), own_sem.at[k])
 
     def gather_start(k):
-        @pl.when(tile_of(k, me) < rounds[k][0])
+        @pl.when(tile_of(k, chip) < rounds[k][0])
         def _():
-            span_wait(k, n_dev - 1, rs_recv, "recv")
+            span_wait(gr.at[k], n_chip - 1, rs_recv.at[k], "recv")
 
             def body(s, total):
                 for i in range(8):
                     total = total + gr[k, s * 8 + i].astype(F32)
                 return total
-            total = lax.fori_loop(0, n_dev // 8, body, jnp.zeros((TILE, LANES), F32))
+            total = lax.fori_loop(0, n_chip // 8, body, jnp.zeros((TILE, LANES), F32))
             ag[k] = total.astype(BF)
             own_copy(k).start()
-            others(lambda d: ag_copy(k, d).start())
+
+            def one(to_g, to_o):
+                pltpu.make_async_remote_copy(
+                    src_ref=ag.at[k], dst_ref=place(k), send_sem=ag_send.at[k],
+                    recv_sem=ag_recv.at[k], device_id=(to_g, to_o), device_id_type=MESH).start()
+            others(one)
 
     def finish(k):
         count = rounds[k][0]
-
-        @pl.when(tile_of(k, me) < count)
+        pair_copy(k).wait_send()
+
+        @pl.when(tile_of(k, chip) < count)
         def _():
             own_copy(k).wait()
-            span_wait(k, count - 1, rs_send, "send")
-            span_wait(k, n_dev - 1, ag_send, "send")
-            at = pl.ds(0, count - 1)
-            pltpu.make_async_remote_copy(
-                src_ref=gall.at[at], dst_ref=gall.at[at], send_sem=ag_send.at[k],
-                recv_sem=ag_recv.at[k], device_id=(g, o), device_id_type=MESH).wait_recv()
-
-        @pl.when(tile_of(k, me) >= count)
+            span_wait(gr.at[k], count - 1, rs_send.at[k], "send")
+            span_wait(gall, n_dev - 1, ag_send.at[k], "send")
+            span_wait(gall, 2 * count - 1, ag_recv.at[k], "recv")
+
+        @pl.when(tile_of(k, chip) >= count)
         def _():
-            span_wait(k, count, rs_send, "send")
-            at = pl.ds(0, count)
-            pltpu.make_async_remote_copy(
-                src_ref=gall.at[at], dst_ref=gall.at[at], send_sem=ag_send.at[k],
-                recv_sem=ag_recv.at[k], device_id=(g, o), device_id_type=MESH).wait_recv()
+            span_wait(gr.at[k], count, rs_send.at[k], "send")
+            span_wait(gall, 2 * count, ag_recv.at[k], "recv")
 
     back_rims(1)
     back_own(1)
     layer_weights(1, act1, gm1, g1)
-    scatter_start(0, g1)
+    pair_copy(0).start()
     gather_messages(1)
+    scatter_start(0)
     add_rims(1)
 
     def back_first(c):
@@ -430,13 +495,13 @@
 
     loop(n_edge // CH, back_first)
     back_rims(0)
+    gather_start(0)
     back_own(0)
     layer_weights(0, act0, gm0, g0)
-    scatter_start(1, g0)
-    gather_start(0)
+    pair_copy(1).start()
+    scatter_start(1)
     add_rims(0)
 
-    ge[0:256, :] = jnp.zeros((256, 256), BF)
     acc[...] = jnp.zeros_like(acc)
 
     def encode_out(c):
@@ -446,7 +511,7 @@
         cemb[at, :] = (mt(rows, enc_out[...]) * edsilu[at, :]).astype(BF)
 
     loop(n_col // CH, encode_out)
-    ge[0:256, :] = acc[...].astype(BF)
+    halves(ge, 0, acc[...])
     acc[...] = jnp.zeros_like(acc)
 
     def encode_in(c):
@@ -454,9 +519,10 @@
         acc[0:128, :] += tm(rx[at, :], cemb[at, :])
 
     loop(n_col // CH, encode_in)
-    ge[256:384, :] = acc[0:128, :].astype(BF)
-    scatter_start(2, ge)
+    halves(ge, 256, acc[0:128, :])
+    pair_copy(2).start()
     gather_start(1)
+    scatter_start(2)
     gather_start(2)
 
     cols_done.wait_send()
@@ -512,7 +578,11 @@
     vm = lambda *shape: pltpu.VMEM(shape, BF)
     vf = lambda *shape: pltpu.VMEM(shape, F32)
     dma = pltpu.SemaphoreType.DMA
-    scratch = [
+    args = (columns, rows(column_live), rows(col_weight), rows(col_slot), node_static, rows(boundary_idx),
+            rows(edge_src), rows(edge_dst), rows(edge_live), rows(edge_weight), enc_in, enc_out, src_proj,
+            dst_proj, msg_proj, node_cotangent)
+    scratch = [pltpu.VMEM(a.shape, a.dtype) for a in args] + [
+        dma((len(args),)), pltpu.SemaphoreType.REGULAR,
         vf(n_dev, LANES), vf(n_dev, LANES), vm(n_col, columns.shape[1]), vf(n_col // LANES, LANES),
         vf(n_col // LANES, LANES), vf(n_col, LANES), vf(n_edge, LANES),
         vm(n_edge, n_node), vm(n_edge, 4 * n_bnd), vm(n_node, n_edge), vm(4 * n_bnd, n_edge),
@@ -524,23 +594,22 @@
         vm(n_edge, width), vm(n_edge, width), vm(n_edge, width), vm(n_edge, width), vm(n_edge, width),
         vf(n_edge, width), vm(n_edge, width), vm(n_node, width), vm(4, n_bnd, width), vm(n_node, width),
         vf(n_node, width),
-        vf(width, width), vm(768, width), vm(768, width), vm(384, width), vm(3, n_dev, TILE, LANES),
-        vm(3, TILE, LANES),
+        vf(width, width), vf(2, 768, LANES), vf(2, 768, LANES), vf(2, 384, LANES),
+        vf(768, LANES), vf(768, LANES), vf(384, LANES), vm(768, LANES), vm(768, LANES), vm(384, LANES),
+        vm(3, n_dev // 2, TILE, LANES), vm(3, TILE, LANES), dma((3,)), dma((3,)),
         dma(()), dma(()), dma(()), dma(()), dma((2, 4)), dma((2, 4)), dma((2, 4)), dma((2, 4)),
         dma((3,)), dma((3,)), dma((3,)), dma((3,)), dma((3,)),
     ]
     in_vmem = pl.BlockSpec(memory_space=pltpu.VMEM)
     node_out, gall = pl.pallas_call(
-        functools.partial(step_kernel, n_grid, n_dom),
+        functools.partial(step_kernel, n_grid, n_dom, len(args)),
         out_shape=(jax.ShapeDtypeStruct((n_node, width), BF), jax.ShapeDtypeStruct((240, TILE, LANES), BF)),
-        in_specs=[in_vmem] * 16,
+        in_specs=[pl.BlockSpec(memory_space=pl.ANY)] * len(args),
         out_specs=(in_vmem, pl.BlockSpec(memory_space=pl.ANY)),
         scratch_shapes=scratch,
         compiler_params=pltpu.CompilerParams(
             collective_id=0, has_side_effects=True, vmem_limit_bytes=62 * 1024 * 1024),
-    )(columns, rows(column_live), rows(col_weight), rows(col_slot), node_static, rows(boundary_idx),
-      rows(edge_src), rows(edge_dst), rows(edge_live), rows(edge_weight), enc_in, enc_out, src_proj,
-      dst_proj, msg_proj, node_cotangent)
+    )(*args)
     mat = jax.ShapeDtypeStruct((width, width), F32)
     pair = jax.ShapeDtypeStruct((2, width, width), F32)
     enc_in_g, enc_out_g, src_g, dst_g, msg_g, node_final = pl.pallas_call(

time: 115 us -> 96 us (0.83)
  Pallas kernels: 114 us -> 95.2 us
    pallas_call x1, Pallas kernels: 111 us -> 92.6 us  [per_device(): pl.pallas_call(functools.partial(step_kernel, n_grid, n_dom, len(args)),...]
where the time goes in v2:
time: 96 us; the launch traced here: 95.9 us
  Pallas kernels  95.2 us (99%)
    pallas_call x1, Pallas kernels, per_device(): pl.pallas_call(functools.partial(step_kernel, n_grid, n_dom, len(args)),...  92.6 us
    pallas_call x1, Pallas kernels, per_device(): pl.pallas_call(finish_kernel, out_shape=(jax.ShapeDtypeStruct(enc_in.shap...  2.63 us

profile of v2, /device:TPU:1, one launch (start us, length us, event | category | flops | bytes accessed | tf_op | source)
XLA Modules:
  0.0 95.9 jit_solution(6205441729272117319)
XLA Ops:
  0.6 92.6 %shard_map.199 = (bf16[512,256]{1,0:T(8,128)(2,1)}, bf16[240,16,128]{2,1,0:T(8,128)(2,1)}) custom-call(bf16[2048,128]{1,0:T(8,128)(2,1)} %refs_0_.1, s32[16,128]{1,0:T(8,128)} %bitcast.8, f32[16,128]{1,0:T(8,128)} %bitcast.9, s32[16,128]{1,0:T(8,128)} %bitcast.10, bf16[512,256]{1,0:T(8,128)(2,1)} %refs_4_.1, s32[2,128]{1,0:T(2,128)} %bitcast.15, ...), custom_call_target="tpu_custom_call" | custom-call | tf_op jit(solution)/shard_map/pallas_call | solution.py:604
  93.2 2.6 %shard_map.200 = (f32[128,256]{1,0:T(8,128)}, f32[256,256]{1,0:T(8,128)}, f32[2,256,256]{2,1,0:T(8,128)}, f32[2,256,256]{2,1,0:T(8,128)}, f32[2,256,256]{2,1,0:T(8,128)}, /*index=5*/bf16[512,256]{1,0:T(8,128)(2,1)}) custom-call(bf16[240,16,128]{2,1,0:T(8,128)(2,1)} %get-tuple-element.14.gall, bf16[512,256]{1,0:T(8,128)(2,1)} %get-tuple-element.15.node_in), custom_call_target="tpu_custom_call" | custom-call | tf_op jit(solution)/shard_map/pallas_call | solution.py:615

commit v3 on v2

--- a/solution.py
+++ b/solution.py
@@ -10,7 +10,8 @@
 MESH = pl.DeviceIdType.MESH
 BF = jnp.bfloat16
 F32 = jnp.float32
-CH = 512
+CH = 1024
+CN = 512
 LANES = 128
 TILE = 16
 
@@ -51,7 +52,7 @@
     so, sr, sot, srt, dd, ddt, bb, bbt, pp, ppt,
     hh, rim, rim_tx, gt_tx, gt_rx,
     eact, edsilu, cemb, pre0, pre1, act0, act1, msg, gm0, gm1, ga1, gp, gs_own, gs_rim, gd, gh,
-    acc, g1, g0, ge, px1, px0, pxe, tx1, tx0, txe, gr, ag,
+    acc, g1, g0, ge, px1, px0, pxe, tx1, tx0, txe, gr, ag, gv, bcol, bdt, bpt, xs, swap_send, swap_recv,
     pair_send, pair_recv,
     a2a_send, a2a_recv, aux_send, aux_recv, rim_send, rim_recv, gt_send, gt_recv,
     rs_send, rs_recv, ag_send, ag_recv, own_sem,
@@ -147,7 +148,7 @@
         pltpu.make_async_remote_copy(
             src_ref=cols.at[pl.ds(pl.multiple_of(d * TILE, TILE), TILE), :],
             dst_ref=rx.at[pl.ds(pl.multiple_of(me * TILE, TILE), TILE), :],
-            send_sem=a2a_send, recv_sem=a2a_recv, device_id=(to_g, to_o), device_id_type=MESH,
+            send_sem=a2a_send, recv_sem=a2a_recv.at[z], device_id=(to_g, to_o), device_id_type=MESH,
         ).start()
 
     others(send_aux)
@@ -182,6 +183,9 @@
             part = slice(c * LANES, (c + 1) * LANES)
             dd[at, part] = hot(down == lane_i + c * LANES)
             ddt[part, at] = hot(full == sub_i + c * LANES)
+        for c in range(n_bnd // LANES):
+            part = slice(c * LANES, (c + 1) * LANES)
+            bdt[part, at] = hot(full == bcol[part, :])
         scale = eweight[pl.ds(b, 1), :] * elive[pl.ds(b, 1), :].astype(F32)
         ecol[at, :] = across(scale)[1]
         full, down = across(esrc[pl.ds(b, 1), :])
@@ -194,8 +198,6 @@
             sr[at, part] = hot(down == lane_i + (n_node + c * LANES))
             srt[part, at] = hot(full == sub_i + (n_node + c * LANES))
 
-    loop(rows_e, build_edges)
-
     def build_bound(b):
         at = pl.ds(pl.multiple_of(b * LANES, LANES), LANES)
         full, down = across(bidx[pl.ds(b, 1), :])
@@ -203,11 +205,16 @@
             part = slice(c * LANES, (c + 1) * LANES)
             bb[at, part] = hot(down == lane_i + c * LANES)
             bbt[part, at] = hot(full == sub_i + c * LANES)
+        bcol[at, :] = down
 
     loop(n_bnd // LANES, build_bound)
+    loop(rows_e, build_edges)
 
     def chunk(c):
         return pl.ds(pl.multiple_of(c * CH, CH), CH)
+
+    def node_chunk(c):
+        return pl.ds(pl.multiple_of(c * CN, CN), CN)
 
     def back_last(c):
         at = chunk(c)
@@ -219,7 +226,7 @@
 
     got = pl.ds(0, (n_dev - 1) * TILE)
     cols_done = pltpu.make_async_remote_copy(
-        src_ref=rx.at[got, :], dst_ref=rx.at[got, :], send_sem=a2a_send, recv_sem=a2a_recv,
+        src_ref=rx.at[got, :], dst_ref=rx.at[got, :], send_sem=a2a_send, recv_sem=a2a_recv.at[0],
         device_id=(g, o), device_id_type=MESH)
     got_aux = pl.ds(0, n_dev - 1)
     aux_done = pltpu.make_async_remote_copy(
@@ -242,16 +249,20 @@
             part = slice(c * LANES, (c + 1) * LANES)
             pp[at, part] = hot(down == lane_f + float(c * LANES))
             ppt[part, at] = hot(full == sub_f + float(c * LANES))
+        for c in range(n_bnd // LANES):
+            part = slice(c * LANES, (c + 1) * LANES)
+            bpt[part, at] = hot(full == bcol[part, :].astype(F32))
         ccol[at, :] = across(crow[pl.ds(b, 1), :])[1]
 
     loop(rows_c, build_pool)
-    cols_done.wait_recv()
 
     def sigmoid(v):
         return 0.5 * jnp.tanh(0.5 * v) + 0.5
 
-    def encode(c):
-        at = chunk(c)
+    plane = n_col // n_z
+
+    def encode(to_z):
+        at = pl.ds(pl.multiple_of(to_z * plane, plane), plane)
         v = mm(rx[at, :], enc_in[...])
         s = sigmoid(v)
         a = (v * s).astype(BF)
@@ -259,13 +270,18 @@
         edsilu[at, :] = s * (1.0 + v * (1.0 - s))
         cemb[at, :] = (mm(a, enc_out[...]) * wide(ccol[at, :])).astype(BF)
 
-    loop(n_col // CH, encode)
+    for dz in reversed(range(n_z)):
+        from_z = lax.rem(z - dz + n_z, n_z)
+        got = pl.ds(0, plane - (TILE if dz == 0 else 0))
+        pltpu.make_async_remote_copy(
+            src_ref=rx.at[got, :], dst_ref=rx.at[got, :], send_sem=a2a_send, recv_sem=a2a_recv.at[from_z],
+            device_id=(g, o), device_id_type=MESH).wait_recv()
+        encode(from_z)
 
     def pool(c):
-        at = chunk(c)
+        at = node_chunk(c)
         hh[0, at, :] = (static[at, :].astype(F32) + mm(ppt[at, :], cemb[...])).astype(BF)
 
-    loop(n_node // CH, pool)
 
     def fwd_copy(l, r):
         return pltpu.make_async_remote_copy(
@@ -278,14 +294,18 @@
             recv_sem=gt_recv.at[l, r], device_id=near[r], device_id_type=MESH)
 
     def send_rims(l):
-        rim_tx[l] = mm(bb[...], hh[l]).astype(BF)
+        if l == 0:
+            rows = mm(bb[...], static[...]) + mm(bpt[...], cemb[...])
+        else:
+            rows = mm(bb[...], hh[0]) + mm(bdt[...], msg[...])
+        rim_tx[l] = rows.astype(BF)
         for r in (2, 3, 0, 1):
             @pl.when(here[flip[r]])
             def _():
                 fwd_copy(l, r).start()
 
-    def wait_rims(l):
-        for r in range(4):
+    def wait_rims(l, blocks):
+        for r in blocks:
             @pl.when(here[r])
             def _():
                 fwd_copy(l, r).wait_recv()
@@ -299,10 +319,17 @@
             pre[at, :] = mm(xo, src_proj[l]) + mm(xd, dst_proj[l])
         loop(n_edge // CH, body)
 
+    def layer_grid(l):
+        def body(c):
+            at = chunk(c)
+            xs[at, :] = mm(sr[at, 0:2 * n_bnd], rim[l, 0:2].reshape(2 * n_bnd, 256)).astype(BF)
+        loop(n_edge // CH, body)
+
     def layer_rest(l, pre, act):
         def body(c):
             at = chunk(c)
-            xr = mm(sr[at, :], rim[l].reshape(4 * n_bnd, 256)).astype(BF)
+            xr = mm(sr[at, 2 * n_bnd:], rim[l, 2:4].reshape(2 * n_bnd, 256))
+            xr = (xr + xs[at, :].astype(F32)).astype(BF)
             v = pre[at, :] + mm(xr, src_proj[l])
             s = sigmoid(v)
             a = (v * s).astype(BF)
@@ -317,22 +344,27 @@
 
     def gather_messages(l):
         def body(c):
-            at = chunk(c)
+            at = node_chunk(c)
             rows = (hh[l, at, :].astype(F32) + mm(ddt[at, :], msg[...])).astype(BF)
             if l == 0:
                 hh[1, at, :] = rows
             else:
                 node_out[at, :] = rows
-        loop(n_node // CH, body)
+        loop(n_node // CN, body)
 
     send_rims(0)
+    loop(n_node // CN, pool)
     layer_own(0, pre0)
-    wait_rims(0)
+    wait_rims(0, (0, 1))
+    layer_grid(0)
+    wait_rims(0, (2, 3))
     layer_rest(0, pre0, act0)
+    send_rims(1)
     gather_messages(0)
-    send_rims(1)
     layer_own(1, pre1)
-    wait_rims(1)
+    wait_rims(1, (0, 1))
+    layer_grid(1)
+    wait_rims(1, (2, 3))
     layer_rest(1, pre1, act1)
 
     def back_rims(l):
@@ -347,14 +379,14 @@
 
     def back_own(l):
         def body(c):
-            at = chunk(c)
+            at = node_chunk(c)
             s_rows = mm(sot[at, :], gp[...]).astype(BF)
             d_rows = mm(ddt[at, :], gp[...]).astype(BF)
             gs_own[at, :] = s_rows
             gd[at, :] = d_rows
             before = cot[at, :].astype(F32) if l == 1 else gh[at, :]
             gh[at, :] = before + mt(s_rows, src_proj[l]) + mt(d_rows, dst_proj[l])
-        loop(n_node // CH, body)
+        loop(n_node // CN, body)
 
     def halves(out, first, value):
         rows = slice(first, first + value.shape[0])
@@ -382,12 +414,12 @@
                 back_copy(l, r).wait_recv()
 
         def body(c):
-            at = chunk(c)
+            at = node_chunk(c)
             total = gh[at, :]
             for r in range(4):
                 total = total + mm(bbt[at, :], gt_rx[l, r])
             gh[at, :] = total
-        loop(n_node // CH, body)
+        loop(n_node // CN, body)
 
     rounds = ((48, 0, 0), (48, 48, 48), (24, 32, 96))
     parts_of = ((g1, px1, tx1), (g0, px0, tx0), (ge, pxe, txe))
@@ -439,45 +471,69 @@
             copy.wait_send()
 
     def place(k):
-        return gall.at[2 * (rounds[k][2] + tile_of(k, chip)) + core]
-
-    def own_copy(k):
-        return pltpu.make_async_copy(ag.at[k], place(k), own_sem.at[k])
+        return gv.at[core, rounds[k][2] + tile_of(k, chip)]
 
     def gather_start(k):
         @pl.when(tile_of(k, chip) < rounds[k][0])
         def _():
             span_wait(gr.at[k], n_chip - 1, rs_recv.at[k], "recv")
 
-            def body(s, total):
-                for i in range(8):
-                    total = total + gr[k, s * 8 + i].astype(F32)
-                return total
-            total = lax.fori_loop(0, n_chip // 8, body, jnp.zeros((TILE, LANES), F32))
-            ag[k] = total.astype(BF)
-            own_copy(k).start()
+            def body(s, totals):
+                return tuple(
+                    totals[i] + gr[k, s * 8 + i].astype(F32) + gr[k, s * 8 + i + 4].astype(F32)
+                    for i in range(4))
+            zero = jnp.zeros((TILE, LANES), F32)
+            totals = lax.fori_loop(0, n_chip // 8, body, (zero,) * 4)
+            total = ((totals[0] + totals[1]) + (totals[2] + totals[3])).astype(BF)
+            ag[k] = total
+            gv[core, rounds[k][2] + tile_of(k, chip)] = total
 
             def one(to_g, to_o):
                 pltpu.make_async_remote_copy(
                     src_ref=ag.at[k], dst_ref=place(k), send_sem=ag_send.at[k],
                     recv_sem=ag_recv.at[k], device_id=(to_g, to_o), device_id_type=MESH).start()
-            others(one)
+            others(one, cores=(0,))
+
+    def swap_copy(k):
+        part = gv.at[core, pl.ds(rounds[k][2], rounds[k][0])]
+        return pltpu.make_async_remote_copy(
+            src_ref=part, dst_ref=part, send_sem=swap_send.at[k], recv_sem=swap_recv.at[k],
+            device_id=(g + 1 - 2 * core, o), device_id_type=MESH)
+
+    def swap_start(k):
+        count = rounds[k][0]
+
+        @pl.when(tile_of(k, chip) < count)
+        def _():
+            span_wait(gr.at[k], count - 1, ag_recv.at[k], "recv")
+
+        @pl.when(tile_of(k, chip) >= count)
+        def _():
+            span_wait(gr.at[k], count, ag_recv.at[k], "recv")
+        swap_copy(k).start()
+
+    def out_copy(k):
+        part = pl.ds(rounds[k][2], rounds[k][0])
+        return pltpu.make_async_copy(gv.at[:, part], gall.at[:, part], own_sem.at[k])
+
+    def out_start(k):
+        swap_copy(k).wait_recv()
+        out_copy(k).start()
 
     def finish(k):
         count = rounds[k][0]
         pair_copy(k).wait_send()
+        swap_copy(k).wait_send()
 
         @pl.when(tile_of(k, chip) < count)
         def _():
-            own_copy(k).wait()
             span_wait(gr.at[k], count - 1, rs_send.at[k], "send")
-            span_wait(gall, n_dev - 1, ag_send.at[k], "send")
-            span_wait(gall, 2 * count - 1, ag_recv.at[k], "recv")
+            span_wait(gr.at[k], n_chip - 1, ag_send.at[k], "send")
 
         @pl.when(tile_of(k, chip) >= count)
         def _():
             span_wait(gr.at[k], count, rs_send.at[k], "send")
-            span_wait(gall, 2 * count, ag_recv.at[k], "recv")
+        out_copy(k).wait()
 
     back_rims(1)
     back_own(1)
@@ -521,9 +577,15 @@
     loop(n_col // CH, encode_in)
     halves(ge, 256, acc[0:128, :])
     pair_copy(2).start()
+    scatter_start(2)
     gather_start(1)
-    scatter_start(2)
+    swap_start(0)
+    out_start(0)
     gather_start(2)
+    swap_start(1)
+    out_start(1)
+    swap_start(2)
+    out_start(2)
 
     cols_done.wait_send()
     aux_done.wait_send()
@@ -540,30 +602,40 @@
         finish(k)
 
 
-def finish_kernel(gall, node_in, enc_in_g, enc_out_g, src_g, dst_g, msg_g, node_out):
-    node_out[...] = node_in[...]
-    layer_refs = (src_g, dst_g, msg_g)
-
-    def put(first, count, store):
-        for t in range(count):
-            rb, half = t // 2, t % 2
-            rows = slice(rb * TILE, (rb + 1) * TILE)
-            store(rows, slice(half * LANES, (half + 1) * LANES), gall[first + t].astype(F32))
-
-    for layer, first in ((1, 0), (0, 96)):
-        for m in range(3):
-            def store(rows, lanes, v, ref=layer_refs[m], layer=layer):
-                ref[layer, rows, lanes] = v
-            put(first + 32 * m, 32, store)
-
-    def store_out(rows, lanes, v):
-        enc_out_g[rows, lanes] = v
-
-    def store_in(rows, lanes, v):
-        enc_in_g[rows, lanes] = v
-
-    put(192, 32, store_out)
-    put(224, 16, store_in)
+def finish_kernel(gall, node_in, enc_in_g, enc_out_g, src_g, dst_g, msg_g, node_out,
+                  tiles, mats, nodes, in_sem, out_sem):
+    jobs = []
+    for layer, first in ((1, 0), (0, 48)):
+        for m, ref in enumerate((src_g, dst_g, msg_g)):
+            jobs.append((first + 16 * m, 16, ref.at[layer]))
+    jobs.append((96, 16, enc_out_g))
+    jobs.append((112, 8, enc_in_g))
+    n = len(jobs)
+
+    def fetch(i):
+        at = pl.ds(jobs[i][0], jobs[i][1])
+        return pltpu.make_async_copy(gall.at[:, at], tiles.at[:, at], in_sem.at[i])
+
+    def put(i):
+        return pltpu.make_async_copy(mats.at[i, pl.ds(0, jobs[i][1] * TILE)], jobs[i][2], out_sem.at[i])
+
+    node_fetch = pltpu.make_async_copy(node_in, nodes, in_sem.at[n])
+    node_put = pltpu.make_async_copy(nodes, node_out, out_sem.at[n])
+    for i in range(n):
+        fetch(i).start()
+    node_fetch.start()
+    for i in range(n):
+        fetch(i).wait()
+        first, count, _ = jobs[i]
+        for half in range(2):
+            block = tiles[half, first:first + count].astype(F32).reshape(count * TILE, LANES)
+            mats[i, 0:count * TILE, half * LANES:(half + 1) * LANES] = block
+        put(i).start()
+    node_fetch.wait()
+    node_put.start()
+    for i in range(n):
+        put(i).wait()
+    node_put.wait()
 
 
 def per_device(n_grid, n_dom, columns, column_live, col_weight, col_slot, node_static, boundary_idx,
@@ -596,14 +668,17 @@
         vf(n_node, width),
         vf(width, width), vf(2, 768, LANES), vf(2, 768, LANES), vf(2, 384, LANES),
         vf(768, LANES), vf(768, LANES), vf(384, LANES), vm(768, LANES), vm(768, LANES), vm(384, LANES),
-        vm(3, n_dev // 2, TILE, LANES), vm(3, TILE, LANES), dma((3,)), dma((3,)),
-        dma(()), dma(()), dma(()), dma(()), dma((2, 4)), dma((2, 4)), dma((2, 4)), dma((2, 4)),
+        vm(3, n_dev // 2, TILE, LANES), vm(3, TILE, LANES), vm(2, 120, TILE, LANES),
+        pltpu.VMEM((n_bnd, LANES), jnp.int32), vm(n_bnd, n_edge), vm(n_bnd, n_col), vm(n_edge, width),
+        dma((3,)), dma((3,)), dma((3,)), dma((3,)),
+        dma(()), dma((n_grid // 2,)), dma(()), dma(()), dma((2, 4)), dma((2, 4)), dma((2, 4)), dma((2, 4)),
         dma((3,)), dma((3,)), dma((3,)), dma((3,)), dma((3,)),
     ]
     in_vmem = pl.BlockSpec(memory_space=pltpu.VMEM)
+    in_hbm = pl.BlockSpec(memory_space=pl.ANY)
     node_out, gall = pl.pallas_call(
         functools.partial(step_kernel, n_grid, n_dom, len(args)),
-        out_shape=(jax.ShapeDtypeStruct((n_node, width), BF), jax.ShapeDtypeStruct((240, TILE, LANES), BF)),
+        out_shape=(jax.ShapeDtypeStruct((n_node, width), BF), jax.ShapeDtypeStruct((2, 120, TILE, LANES), BF)),
         in_specs=[pl.BlockSpec(memory_space=pl.ANY)] * len(args),
         out_specs=(in_vmem, pl.BlockSpec(memory_space=pl.ANY)),
         scratch_shapes=scratch,
@@ -616,8 +691,9 @@
         finish_kernel,
         out_shape=(jax.ShapeDtypeStruct(enc_in.shape, F32), mat, pair, pair, pair,
                    jax.ShapeDtypeStruct((n_node, width), BF)),
-        in_specs=[in_vmem] * 2,
-        out_specs=(in_vmem,) * 6,
+        in_specs=[in_hbm] * 2,
+        out_specs=(in_hbm,) * 6,
+        scratch_shapes=[vm(2, 120, TILE, LANES), vf(8, width, width), vm(n_node, width), dma((9,)), dma((9,))],
     )(gall, node_out)
     return (node_final, enc_in_g, enc_out_g, src_g, dst_g, msg_g)
 

time: 96 us -> 85.9 us (0.89)
  Pallas kernels: 95.2 us -> 84.9 us
    pallas_call x1, Pallas kernels: 92.6 us -> 82.5 us  [per_device(): pl.pallas_call(functools.partial(step_kernel, n_grid, n_dom, len(args)),...]
where the time goes in v3:
time: 85.9 us; the launch traced here: 85.7 us
  Pallas kernels  84.9 us (99%)
    pallas_call x1, Pallas kernels, per_device(): pl.pallas_call(functools.partial(step_kernel, n_grid, n_dom, len(args)),...  82.5 us
    pallas_call x1, Pallas kernels, per_device(): pl.pallas_call(finish_kernel, out_shape=(jax.ShapeDtypeStruct(enc_in.shap...  2.43 us

profile of v3, /device:TPU:1, one launch (start us, length us, event | category | flops | bytes accessed | tf_op | source)
XLA Modules:
  0.0 85.7 jit_solution(8832922236997021972)
XLA Ops:
  0.6 82.5 %shard_map.199 = (bf16[512,256]{1,0:T(8,128)(2,1)}, bf16[2,120,16,128]{3,2,1,0:T(8,128)(2,1)}) custom-call(bf16[2048,128]{1,0:T(8,128)(2,1)} %refs_0_.1, s32[16,128]{1,0:T(8,128)} %bitcast.8, f32[16,128]{1,0:T(8,128)} %bitcast.9, s32[16,128]{1,0:T(8,128)} %bitcast.10, bf16[512,256]{1,0:T(8,128)(2,1)} %refs_4_.1, s32[2,128]{1,0:T(2,128)} %bitcast.15, ...), custom_call_target="tpu_custom_call" | custom-call | tf_op jit(solution)/shard_map/pallas_call | solution.py:679
  83.1 2.4 %shard_map.200 = (f32[128,256]{1,0:T(8,128)}, f32[256,256]{1,0:T(8,128)}, f32[2,256,256]{2,1,0:T(8,128)}, f32[2,256,256]{2,1,0:T(8,128)}, f32[2,256,256]{2,1,0:T(8,128)}, /*index=5*/bf16[512,256]{1,0:T(8,128)(2,1)}) custom-call(bf16[2,120,16,128]{3,2,1,0:T(8,128)(2,1)} %get-tuple-element.14.gall, bf16[512,256]{1,0:T(8,128)(2,1)} %get-tuple-element.15.node_in), custom_call_target="tpu_custom_call" | custom-call | tf_op jit(solution)/shard_map/pallas_call | solution.py:690

commit v4 on v3

--- a/solution.py
+++ b/solution.py
@@ -41,18 +41,18 @@
     n_in, *refs,
 ):
     inputs = refs[:n_in]
-    node_out, gall = refs[n_in:n_in + 2]
-    copies = refs[n_in + 2:2 * n_in + 2]
-    step_body(n_grid, n_dom, inputs, copies, node_out, gall, *refs[2 * n_in + 2:])
+    outs = refs[n_in:n_in + 3]
+    copies = refs[n_in + 3:2 * n_in + 3]
+    step_body(n_grid, n_dom, inputs, copies, *outs, *refs[2 * n_in + 3:])
 
 
 def step_body(
-    n_grid, n_dom, inputs, copies, node_out, gall,
+    n_grid, n_dom, inputs, copies, node_out, gall, gall_enc,
     in_sem, round_sem, aux_tx, aux_rx, rx, srow, crow, ccol, ecol,
     so, sr, sot, srt, dd, ddt, bb, bbt, pp, ppt,
     hh, rim, rim_tx, gt_tx, gt_rx,
     eact, edsilu, cemb, pre0, pre1, act0, act1, msg, gm0, gm1, ga1, gp, gs_own, gs_rim, gd, gh,
-    acc, g1, g0, ge, px1, px0, pxe, tx1, tx0, txe, gr, ag, gv, bcol, bdt, bpt, xs, swap_send, swap_recv,
+    acc, g1, g0, ge, px1, px0, pxe, tx1, tx0, txe, gr, gre, ag, age, gv, bcol, bdt, bpt, xs, swap_send, swap_recv,
     pair_send, pair_recv,
     a2a_send, a2a_recv, aux_send, aux_recv, rim_send, rim_recv, gt_send, gt_recv,
     rs_send, rs_recv, ag_send, ag_recv, own_sem,
@@ -334,13 +334,22 @@
             s = sigmoid(v)
             a = (v * s).astype(BF)
             act[at, :] = a
-            slope = s * (1.0 + v * (1.0 - s))
             if l == 0:
-                pre[at, :] = slope
+                pre[at, :] = v
+                msg[at, :] = (mm(a, msg_proj[l]) * wide(ecol[at, :])).astype(BF)
             else:
-                gp[at, :] = (ga1[at, :] * slope).astype(BF)
-            msg[at, :] = (mm(a, msg_proj[l]) * wide(ecol[at, :])).astype(BF)
+                gp[at, :] = (ga1[at, :] * (s * (1.0 + v * (1.0 - s)))).astype(BF)
         loop(n_edge // CH, body)
+
+    def slopes(c):
+        at = chunk(c)
+        v = pre0[at, :]
+        s = sigmoid(v)
+        pre0[at, :] = s * (1.0 + v * (1.0 - s))
+
+    def last_messages(c):
+        at = chunk(c)
+        msg[at, :] = (mm(act1[at, :], msg_proj[1]) * wide(ecol[at, :])).astype(BF)
 
     def gather_messages(l):
         def body(c):
@@ -421,7 +430,7 @@
             gh[at, :] = total
         loop(n_node // CN, body)
 
-    rounds = ((48, 0, 0), (48, 48, 48), (24, 32, 96))
+    rounds = ((48, 0, 0), (48, 48, 48), (48, 16, 0))
     parts_of = ((g1, px1, tx1), (g0, px0, tx0), (ge, pxe, txe))
 
     def tile_of(k, q):
@@ -436,15 +445,25 @@
     def rows_of(t):
         return pl.ds(pl.multiple_of(t * TILE, TILE), TILE)
 
+    def held(k):
+        return gre if k == 2 else gr.at[k]
+
     def scatter_start(k):
+        def tile(ref, t):
+            return ref.at[t] if k == 2 else ref.at[rows_of(t), :]
+
         count = rounds[k][0]
         mine, theirs, out = parts_of[k]
         pair_copy(k).wait_recv()
 
         def add(c):
             at = pl.ds(pl.multiple_of(c * LANES, LANES), LANES)
-            out[at, :] = (mine[core, at, :] + theirs[at, :]).astype(BF)
-        loop(out.shape[0] // LANES, add)
+            total = mine[core, at, :] + theirs[at, :]
+            if k < 2:
+                out[at, :] = total.astype(BF)
+            else:
+                out[pl.ds(c * 16, 16)] = total.reshape(16, 8, LANES).astype(BF)
+        loop(theirs.shape[0] // LANES, add)
 
         def one(to_g, to_o):
             t = tile_of(k, (to_g // 2) * n_dom + to_o)
@@ -452,13 +471,13 @@
             @pl.when(t < count)
             def _():
                 pltpu.make_async_remote_copy(
-                    src_ref=out.at[rows_of(t), :], dst_ref=gr.at[k, chip], send_sem=rs_send.at[k],
+                    src_ref=tile(out, t), dst_ref=held(k).at[chip], send_sem=rs_send.at[k],
                     recv_sem=rs_recv.at[k], device_id=(to_g, to_o), device_id_type=MESH).start()
         others(one, cores=(0,))
 
         @pl.when(tile_of(k, chip) < count)
         def _():
-            gr[k, chip] = out[rows_of(tile_of(k, chip)), :]
+            held(k)[chip] = tile(out, tile_of(k, chip))[...]
 
     def span_wait(ref, n, sem, what):
         at = pl.ds(0, n)
@@ -471,28 +490,39 @@
             copy.wait_send()
 
     def place(k):
+        if k == 2:
+            return gall_enc.at[core, tile_of(k, chip)]
         return gv.at[core, rounds[k][2] + tile_of(k, chip)]
+
+    def own_copy():
+        return pltpu.make_async_copy(age, place(2), own_sem.at[2])
 
     def gather_start(k):
         @pl.when(tile_of(k, chip) < rounds[k][0])
         def _():
-            span_wait(gr.at[k], n_chip - 1, rs_recv.at[k], "recv")
+            span_wait(held(k), n_chip - 1, rs_recv.at[k], "recv")
 
             def body(s, totals):
                 return tuple(
-                    totals[i] + gr[k, s * 8 + i].astype(F32) + gr[k, s * 8 + i + 4].astype(F32)
+                    totals[i] + held(k)[s * 8 + i].astype(F32) + held(k)[s * 8 + i + 4].astype(F32)
                     for i in range(4))
-            zero = jnp.zeros((TILE, LANES), F32)
+            zero = jnp.zeros((8 if k == 2 else TILE, LANES), F32)
             totals = lax.fori_loop(0, n_chip // 8, body, (zero,) * 4)
             total = ((totals[0] + totals[1]) + (totals[2] + totals[3])).astype(BF)
-            ag[k] = total
-            gv[core, rounds[k][2] + tile_of(k, chip)] = total
+            if k < 2:
+                ag[k] = total
+                gv[core, rounds[k][2] + tile_of(k, chip)] = total
+                source = ag.at[k]
+            else:
+                age[...] = total
+                source = age
+                own_copy().start()
 
             def one(to_g, to_o):
                 pltpu.make_async_remote_copy(
-                    src_ref=ag.at[k], dst_ref=place(k), send_sem=ag_send.at[k],
+                    src_ref=source, dst_ref=place(k), send_sem=ag_send.at[k],
                     recv_sem=ag_recv.at[k], device_id=(to_g, to_o), device_id_type=MESH).start()
-            others(one, cores=(0,))
+            others(one, cores=(0,) if k < 2 else (1, 0))
 
     def swap_copy(k):
         part = gv.at[core, pl.ds(rounds[k][2], rounds[k][0])]
@@ -520,6 +550,22 @@
         swap_copy(k).wait_recv()
         out_copy(k).start()
 
+    def finish_enc():
+        count = rounds[2][0]
+        pair_copy(2).wait_send()
+
+        @pl.when(tile_of(2, chip) < count)
+        def _():
+            own_copy().wait()
+            span_wait(gre, count - 1, rs_send.at[2], "send")
+            span_wait(gre, n_dev - 1, ag_send.at[2], "send")
+            span_wait(gre, 2 * count - 1, ag_recv.at[2], "recv")
+
+        @pl.when(tile_of(2, chip) >= count)
+        def _():
+            span_wait(gre, count, rs_send.at[2], "send")
+            span_wait(gre, 2 * count, ag_recv.at[2], "recv")
+
     def finish(k):
         count = rounds[k][0]
         pair_copy(k).wait_send()
@@ -539,8 +585,10 @@
     back_own(1)
     layer_weights(1, act1, gm1, g1)
     pair_copy(0).start()
+    loop(n_edge // CH, slopes)
+    scatter_start(0)
+    loop(n_edge // CH, last_messages)
     gather_messages(1)
-    scatter_start(0)
     add_rims(1)
 
     def back_first(c):
@@ -584,8 +632,6 @@
     gather_start(2)
     swap_start(1)
     out_start(1)
-    swap_start(2)
-    out_start(2)
 
     cols_done.wait_send()
     aux_done.wait_send()
@@ -598,26 +644,29 @@
             @pl.when(here[r])
             def _():
                 back_copy(l, r).wait_send()
-    for k in range(3):
+    for k in range(2):
         finish(k)
-
-
-def finish_kernel(gall, node_in, enc_in_g, enc_out_g, src_g, dst_g, msg_g, node_out,
-                  tiles, mats, nodes, in_sem, out_sem):
+    finish_enc()
+
+
+def finish_kernel(gall, gall_enc, node_in, enc_in_g, enc_out_g, src_g, dst_g, msg_g, node_out,
+                  tiles, tiles_enc, mats, nodes, in_sem, out_sem):
     jobs = []
     for layer, first in ((1, 0), (0, 48)):
         for m, ref in enumerate((src_g, dst_g, msg_g)):
-            jobs.append((first + 16 * m, 16, ref.at[layer]))
-    jobs.append((96, 16, enc_out_g))
-    jobs.append((112, 8, enc_in_g))
+            jobs.append((gall, tiles, first + 16 * m, 16, ref.at[layer]))
+    jobs.append((gall_enc, tiles_enc, 0, 32, enc_out_g))
+    jobs.append((gall_enc, tiles_enc, 32, 16, enc_in_g))
     n = len(jobs)
 
     def fetch(i):
-        at = pl.ds(jobs[i][0], jobs[i][1])
-        return pltpu.make_async_copy(gall.at[:, at], tiles.at[:, at], in_sem.at[i])
+        source, held, first, count, _ = jobs[i]
+        at = pl.ds(first, count)
+        return pltpu.make_async_copy(source.at[:, at], held.at[:, at], in_sem.at[i])
 
     def put(i):
-        return pltpu.make_async_copy(mats.at[i, pl.ds(0, jobs[i][1] * TILE)], jobs[i][2], out_sem.at[i])
+        target = jobs[i][4]
+        return pltpu.make_async_copy(mats.at[i, pl.ds(0, target.shape[0])], target, out_sem.at[i])
 
     node_fetch = pltpu.make_async_copy(node_in, nodes, in_sem.at[n])
     node_put = pltpu.make_async_copy(nodes, node_out, out_sem.at[n])
@@ -626,10 +675,11 @@
     node_fetch.start()
     for i in range(n):
         fetch(i).wait()
-        first, count, _ = jobs[i]
+        _, held, first, count, target = jobs[i]
+        n_row = target.shape[0]
         for half in range(2):
-            block = tiles[half, first:first + count].astype(F32).reshape(count * TILE, LANES)
-            mats[i, 0:count * TILE, half * LANES:(half + 1) * LANES] = block
+            block = held[half, first:first + count].astype(F32).reshape(n_row, LANES)
+            mats[i, 0:n_row, half * LANES:(half + 1) * LANES] = block
         put(i).start()
     node_fetch.wait()
     node_put.start()
@@ -667,8 +717,9 @@
         vf(n_edge, width), vm(n_edge, width), vm(n_node, width), vm(4, n_bnd, width), vm(n_node, width),
         vf(n_node, width),
         vf(width, width), vf(2, 768, LANES), vf(2, 768, LANES), vf(2, 384, LANES),
-        vf(768, LANES), vf(768, LANES), vf(384, LANES), vm(768, LANES), vm(768, LANES), vm(384, LANES),
-        vm(3, n_dev // 2, TILE, LANES), vm(3, TILE, LANES), vm(2, 120, TILE, LANES),
+        vf(768, LANES), vf(768, LANES), vf(384, LANES), vm(768, LANES), vm(768, LANES), vm(48, 8, LANES),
+        vm(2, n_dev // 2, TILE, LANES), vm(n_dev, 8, LANES), vm(2, TILE, LANES), vm(8, LANES),
+        vm(2, 96, TILE, LANES),
         pltpu.VMEM((n_bnd, LANES), jnp.int32), vm(n_bnd, n_edge), vm(n_bnd, n_col), vm(n_edge, width),
         dma((3,)), dma((3,)), dma((3,)), dma((3,)),
         dma(()), dma((n_grid // 2,)), dma(()), dma(()), dma((2, 4)), dma((2, 4)), dma((2, 4)), dma((2, 4)),
@@ -676,11 +727,12 @@
     ]
     in_vmem = pl.BlockSpec(memory_space=pltpu.VMEM)
     in_hbm = pl.BlockSpec(memory_space=pl.ANY)
-    node_out, gall = pl.pallas_call(
+    node_out, gall, gall_enc = pl.pallas_call(
         functools.partial(step_kernel, n_grid, n_dom, len(args)),
-        out_shape=(jax.ShapeDtypeStruct((n_node, width), BF), jax.ShapeDtypeStruct((2, 120, TILE, LANES), BF)),
+        out_shape=(jax.ShapeDtypeStruct((n_node, width), BF), jax.ShapeDtypeStruct((2, 96, TILE, LANES), BF),
+                   jax.ShapeDtypeStruct((2, 48, 8, LANES), BF)),
         in_specs=[pl.BlockSpec(memory_space=pl.ANY)] * len(args),
-        out_specs=(in_vmem, pl.BlockSpec(memory_space=pl.ANY)),
+        out_specs=(in_vmem, in_hbm, in_hbm),
         scratch_shapes=scratch,
         compiler_params=pltpu.CompilerParams(
             collective_id=0, has_side_effects=True, vmem_limit_bytes=62 * 1024 * 1024),
@@ -691,10 +743,10 @@
         finish_kernel,
         out_shape=(jax.ShapeDtypeStruct(enc_in.shape, F32), mat, pair, pair, pair,
                    jax.ShapeDtypeStruct((n_node, width), BF)),
-        in_specs=[in_hbm] * 2,
+        in_specs=[in_hbm] * 3,
         out_specs=(in_hbm,) * 6,
-        scratch_shapes=[vm(2, 120, TILE, LANES), vf(8, width, width), vm(n_node, width), dma((9,)), dma((9,))],
-    )(gall, node_out)
+        scratch_shapes=[vm(2, 96, TILE, LANES), vm(2, 48, 8, LANES), vf(8, width, width), vm(n_node, width), dma((9,)), dma((9,))],
+    )(gall, gall_enc, node_out)
     return (node_final, enc_in_g, enc_out_g, src_g, dst_g, msg_g)
 
 

time: 85.9 us -> 83.9 us (0.977)
  Pallas kernels: 84.9 us -> 83 us
    pallas_call x1, Pallas kernels: 82.5 us -> 80.5 us  [per_device(): pl.pallas_call(functools.partial(step_kernel, n_grid, n_dom, len(args)),...]
where the time goes in v4:
time: 83.9 us; the launch traced here: 83.8 us
  Pallas kernels  83 us (99%)
    pallas_call x1, Pallas kernels, per_device(): pl.pallas_call(functools.partial(step_kernel, n_grid, n_dom, len(args)),...  80.5 us
    pallas_call x1, Pallas kernels, per_device(): pl.pallas_call(finish_kernel, out_shape=(jax.ShapeDtypeStruct(enc_in.shap...  2.43 us

profile of v4, /device:TPU:1, one launch (start us, length us, event | category | flops | bytes accessed | tf_op | source)
XLA Modules:
  0.0 83.8 jit_solution(2655086024003780963)
XLA Ops:
  0.6 80.5 %shard_map.199 = (bf16[512,256]{1,0:T(8,128)(2,1)}, bf16[2,96,16,128]{3,2,1,0:T(8,128)(2,1)}, bf16[2,48,8,128]{3,2,1,0:T(8,128)(2,1)}) custom-call(bf16[2048,128]{1,0:T(8,128)(2,1)} %refs_0_.1, s32[16,128]{1,0:T(8,128)} %bitcast.8, f32[16,128]{1,0:T(8,128)} %bitcast.9, s32[16,128]{1,0:T(8,128)} %bitcast.10, bf16[512,256]{1,0:T(8,128)(2,1)} %refs_4_.1, ...), custom_call_target="tpu_custom_call" | custom-call | tf_op jit(solution)/shard_map/pallas_call | solution.py:730
  81.2 2.4 %shard_map.200 = (f32[128,256]{1,0:T(8,128)}, f32[256,256]{1,0:T(8,128)}, f32[2,256,256]{2,1,0:T(8,128)}, f32[2,256,256]{2,1,0:T(8,128)}, f32[2,256,256]{2,1,0:T(8,128)}, /*index=5*/bf16[512,256]{1,0:T(8,128)(2,1)}) custom-call(bf16[2,96,16,128]{3,2,1,0:T(8,128)(2,1)} %get-tuple-element.15.gall, bf16[2,48,8,128]{3,2,1,0:T(8,128)(2,1)} %get-tuple-element.16.gall_enc, ...), custom_call_target="tpu_custom_call" | custom-call | tf_op jit(solution)/shard_map/pallas_call | solution.py:742

commit v5 on v4

--- a/solution.py
+++ b/solution.py
@@ -599,10 +599,10 @@
 
     loop(n_edge // CH, back_first)
     back_rims(0)
-    gather_start(0)
     back_own(0)
     layer_weights(0, act0, gm0, g0)
     pair_copy(1).start()
+    gather_start(0)
     scatter_start(1)
     add_rims(0)
 

time: 83.9 us -> 83 us (0.989)
  Pallas kernels: 83 us -> 82.1 us
    pallas_call x1, Pallas kernels: 80.5 us -> 79.6 us  [per_device(): pl.pallas_call(functools.partial(step_kernel, n_grid, n_dom, len(args)),...]
where the time goes in v5:
time: 83 us; the launch traced here: 82.9 us
  Pallas kernels  82.1 us (99%)
    pallas_call x1, Pallas kernels, per_device(): pl.pallas_call(functools.partial(step_kernel, n_grid, n_dom, len(args)),...  79.6 us
    pallas_call x1, Pallas kernels, per_device(): pl.pallas_call(finish_kernel, out_shape=(jax.ShapeDtypeStruct(enc_in.shap...  2.43 us

profile of v5, /device:TPU:1, one launch (start us, length us, event | category | flops | bytes accessed | tf_op | source)
XLA Modules:
  0.0 82.9 jit_solution(13820636179072951910)
XLA Ops:
  0.6 79.6 %shard_map.199 = (bf16[512,256]{1,0:T(8,128)(2,1)}, bf16[2,96,16,128]{3,2,1,0:T(8,128)(2,1)}, bf16[2,48,8,128]{3,2,1,0:T(8,128)(2,1)}) custom-call(bf16[2048,128]{1,0:T(8,128)(2,1)} %refs_0_.1, s32[16,128]{1,0:T(8,128)} %bitcast.8, f32[16,128]{1,0:T(8,128)} %bitcast.9, s32[16,128]{1,0:T(8,128)} %bitcast.10, bf16[512,256]{1,0:T(8,128)(2,1)} %refs_4_.1, ...), custom_call_target="tpu_custom_call" | custom-call | tf_op jit(solution)/shard_map/pallas_call | solution.py:730
  80.3 2.4 %shard_map.200 = (f32[128,256]{1,0:T(8,128)}, f32[256,256]{1,0:T(8,128)}, f32[2,256,256]{2,1,0:T(8,128)}, f32[2,256,256]{2,1,0:T(8,128)}, f32[2,256,256]{2,1,0:T(8,128)}, /*index=5*/bf16[512,256]{1,0:T(8,128)(2,1)}) custom-call(bf16[2,96,16,128]{3,2,1,0:T(8,128)(2,1)} %get-tuple-element.15.gall, bf16[2,48,8,128]{3,2,1,0:T(8,128)(2,1)} %get-tuple-element.16.gall_enc, ...), custom_call_target="tpu_custom_call" | custom-call | tf_op jit(solution)/shard_map/pallas_call | solution.py:742
